TPU v7x, 32 devices: a whole 2x2x4 slice. The times are simulated.
32 devices in a mesh: replica: 8 (over y, x, core), model: 4 (over z).
Axes of the slice: x: 2, y: 2, z: 4, core: 2. Of those that a mesh axis runs over, the one named last changes fastest.
Arguments:
- slope_gate: float32 [8, 2048, 6144], P('replica', None, 'model'), may hold values from -0.875 to 0.875
- slope_up: float32 [8, 2048, 6144], P('replica', None, 'model'), may hold values from -0.875 to 0.875
- slope_down: float32 [8, 6144, 2048], P('replica', 'model'), may hold values from -0.875 to 0.875
- slope_norm: float32 [8, 2048], P('replica'), may hold values from -8 to 8
- param_gate: float32 [2048, 6144], P('replica', 'model'), may hold values from -0.1875 to 0.1875
- param_up: float32 [2048, 6144], P('replica', 'model'), may hold values from -0.1875 to 0.1875
- param_down: float32 [6144, 2048], P('model', 'replica'), may hold values from -0.109375 to 0.109375
- param_norm: float32 [2048], P('replica'), may hold values from 0.25 to 1.75
Outputs:
- half_gate: bfloat16 [2048, 6144], P(None, 'model')
- half_up: bfloat16 [2048, 6144], P(None, 'model')
- half_down: bfloat16 [6144, 2048], P('model')
- half_norm: bfloat16 [2048], replicated
- next_gate: float32 [2048, 6144], P('replica', 'model')
- next_up: float32 [2048, 6144], P('replica', 'model')
- next_down: float32 [6144, 2048], P('model', 'replica')
- next_norm: float32 [2048], P('replica')
All inputs are finite; a program needn't handle non-finite values.
Results may differ from a plain program's by a relative error of at most 0.0004.
Values may be sent and summed in bfloat16 or wider, within the bound.
A program may use at most 128 MiB of HBM per device.

v0:
```python
import functools

import jax
import jax.numpy as jnp
from jax import lax
from jax.experimental import pallas as pl
from jax.experimental.pallas import tpu as pltpu
from jax.sharding import PartitionSpec as P

learn_rate = 0.5
eps = 1e-06
MESH = pl.DeviceIdType.MESH
f32, bf16 = jnp.float32, jnp.bfloat16
PIECES = 2
SLOTS = 4


def tile_rows(columns, most=12288):
    return 8 * max(1, most // (8 * columns))


def kernel(
    replicas, models,
    g_ref, u_ref, d_ref, nv_ref, pg_ref, pu_ref, pd_ref,
    hg_ref, hu_ref, hd_ref, ng_ref, nu_ref, nd_ref, hn_ref, nn_ref,
    pr_g, pr_u, pr_d, r1_g, r1_u, r1_d, r2_g, r2_u, r2_d,
    ow_w, ow_d, hb_g, hb_u, hb_d, nrm_w, nrm_d, zr_w, zr_d, nr, whole,
    ow_sem, pr_send, pr_recv, s1_send, s1_recv, s2_send, s2_recv,
    z_send, z_recv, n_send, n_recv, ag_send, ag_recv, loc_sem, next_sem,
):
    me = lax.axis_index("replica")
    z = lax.axis_index("model")
    k = lax.rem(me, 2)
    x = lax.rem(me // 2, 2)
    y = me // 4
    partner = me + 1 - 2 * k
    xn = me + 2 - 4 * x
    yn = me + 4 - 8 * y
    rate = replicas ** (-0.5)

    slopes = (g_ref, u_ref, d_ref)
    params = (pg_ref, pu_ref, pd_ref)
    halves = (hg_ref, hu_ref, hd_ref)
    nexts = (ng_ref, nu_ref, nd_ref)
    pr, r1, r2 = (pr_g, pr_u, pr_d), (r1_g, r1_u, r1_d), (r2_g, r2_u, r2_d)
    hb = (hb_g, hb_u, hb_d)
    units = 2 * PIECES
    side = pd_ref.shape[1]

    others = [lax.rem(me + d, replicas) for d in range(1, replicas)]
    layers = [lax.rem(z + d, models) for d in range(1, models)]
    barrier = pltpu.get_barrier_semaphore()
    for other in others:
        pl.semaphore_signal(barrier, inc=1, device_id=(other, z), device_id_type=MESH)
    for layer in layers:
        pl.semaphore_signal(barrier, inc=1, device_id=(me, layer), device_id_type=MESH)
    pl.semaphore_wait(barrier, replicas - 1 + models - 1)

    sent = []

    def remote(src, dst, send_sem, recv_sem, to):
        return pltpu.make_async_remote_copy(
            src_ref=src, dst_ref=dst, send_sem=send_sem, recv_sem=recv_sem,
            device_id=to, device_id_type=MESH,
        )

    def start(copy):
        copy.start()
        sent.append(copy)

    def height(m):
        return r2[m].shape[0] // units

    def views(m, u, core):
        rows = pl.ds(u * height(m), height(m))
        if m < 2:
            return [(slopes[m].at[:, :, core, rows, :], None)]
        return [
            (
                slopes[m].at[
                    rows, pl.ds(pl.multiple_of((2 * c + core) * side, side), side)
                ],
                (c // 2, c % 2),
            )
            for c in range(4)
        ]

    def own_copies(m, u):
        ow = ow_w if m < 2 else ow_d
        slot = (m * units + order[u]) % SLOTS
        copies = []
        for n, (src, where) in enumerate(views(m, u, k)):
            dst = ow.at[slot] if where is None else ow.at[slot, where[0], where[1]]
            copies.append(pltpu.make_async_copy(src, dst, ow_sem.at[m, u, n]))
        return copies

    def pair_copies(m, u):
        copies = []
        for n, (src, where) in enumerate(views(m, u, 1 - k)):
            dst = pr[m].at[u] if where is None else pr[m].at[u, where[0], where[1]]
            copies.append(
                remote(src, dst, pr_send.at[m, u, n], pr_recv.at[m, u, n], (partner, z))
            )
        return copies

    sequence = [h * PIECES + j for j in range(PIECES) for h in range(2)]
    order = {u: n for n, u in enumerate(sequence)}
    jobs = [(m, u) for m in range(3) for u in sequence]

    for m, u in jobs[:SLOTS]:
        for copy in own_copies(m, u):
            copy.start()
    for m, u in jobs:
        for copy in pair_copies(m, u):
            start(copy)
    nr[me] = nv_ref[...]
    for n, other in enumerate(others):
        start(remote(nv_ref, nr.at[me], n_send.at[n], n_recv.at[me], (other, z)))

    def first_copy(m, u):
        if u < PIECES:
            src, to = pr[m].at[u, :, 1 - x], xn
        else:
            src, to = pr[m].at[u, 1 - y], yn
        return remote(src, r1[m].at[u], s1_send.at[m, u], s1_recv.at[m, u], (to, z))

    def second_copy(m, u):
        if u < PIECES:
            src, to = r1[m].at[u, 1 - y], yn
        else:
            src, to = r1[m].at[u, 1 - x], xn
        rows = pl.ds(u * height(m), height(m))
        return remote(src, r2[m].at[rows], s2_send.at[m, u], s2_recv.at[m, u], (to, z))

    def stage_1(n):
        m, u = jobs[n]
        ow = ow_w if m < 2 else ow_d
        slot = n % SLOTS
        for copy in own_copies(m, u):
            copy.wait()
        for copy in pair_copies(m, u):
            copy.wait_recv()
        step = tile_rows(r2[m].shape[1])

        @pl.loop(0, height(m) // step)
        def _(i):
            rows = pl.ds(pl.multiple_of(i * step, step), step)
            for a in range(2):
                for b in range(2):
                    pr[m][u, a, b, rows, :] = pr[m][u, a, b, rows, :] + ow[slot, a, b, rows, :]

        start(first_copy(m, u))
        if n + SLOTS < len(jobs):
            for copy in own_copies(*jobs[n + SLOTS]):
                copy.start()

    def stage_2(n):
        m, u = jobs[n]
        first_copy(m, u).wait_recv()
        step = tile_rows(r2[m].shape[1])

        @pl.loop(0, height(m) // step)
        def _(i):
            rows = pl.ds(pl.multiple_of(i * step, step), step)
            for a in range(2):
                kept = pr[m][u, a, x, rows, :] if u < PIECES else pr[m][u, y, a, rows, :]
                r1[m][u, a, rows, :] = r1[m][u, a, rows, :] + kept

        start(second_copy(m, u))

    def lanes(t):
        total = t[:, :128]
        for c in range(1, t.shape[1] // 128):
            total = total + t[:, c * 128 : (c + 1) * 128]
        return total

    def sublanes(t):
        total = t[:8]
        for c in range(1, t.shape[0] // 8):
            total = total + t[c * 8 : (c + 1) * 8]
        return total

    def stage_3(n):
        m, u = jobs[n]
        second_copy(m, u).wait_recv()
        step = tile_rows(r2[m].shape[1])
        kept = y if u < PIECES else x
        if m == 2 and u == sequence[0]:
            nrm_d[...] = jnp.zeros_like(nrm_d)

        @pl.loop(0, height(m) // step)
        def _(i):
            rows = pl.ds(pl.multiple_of(i * step, step), step)
            here = pl.ds(pl.multiple_of(u * height(m) + i * step, step), step)
            mean = (r2[m][here, :] + r1[m][u, kept, rows, :]) * rate
            param = params[m][here, :]
            r2[m][here, :] = mean
            if m < 2:
                nrm_w[m, 0, here, :] = lanes(param * param)
                nrm_w[m, 1, here, :] = lanes(mean * mean)
            else:
                nrm_d[0] = nrm_d[0] + sublanes(param * param)
                nrm_d[1] = nrm_d[1] + sublanes(mean * mean)

    def size_copies(m):
        src = nrm_w.at[m] if m < 2 else nrm_d
        return [
            remote(
                src, zr_w.at[m, n] if m < 2 else zr_d.at[n],
                z_send.at[m, n], z_recv.at[m, n], (me, layer),
            )
            for n, layer in enumerate(layers)
        ]

    def send_sizes(m):
        for copy in size_copies(m):
            start(copy)

    def piece(m, chip, core, h):
        ref = halves[m]
        at = pl.multiple_of((2 * chip + core) * r2[0].shape[0], r2[0].shape[0])
        if m < 2:
            tall = r2[m].shape[0] // 2
            return ref.at[pl.ds(pl.multiple_of(at + h * tall, tall), tall), :]
        tall = r2[m].shape[0] // 2
        at = pl.multiple_of((2 * chip + core) * side, side)
        return ref.at[pl.ds(h * tall, tall), pl.ds(at, side)]

    chip, chip_x, chip_y, chip_d = me // 2, xn // 2, yn // 2, 3 - me // 2

    def gather(m, h, way, src, at, to):
        return remote(src, at, ag_send.at[m, h, way], ag_recv.at[m, h, way], (to, z))

    def await_piece(m, h, way, chip_from, core):
        at = piece(m, chip_from, core, h)
        gather(m, h, way, at, at, partner).wait_recv()
        return at

    local = []

    def update(m):
        for copy in size_copies(m):
            copy.wait_recv()
        step = tile_rows(r2[m].shape[1])
        if m == 2:
            both = nrm_d[...]
            for n in range(models - 1):
                both = both + zr_d[n]
            own = jnp.sum(both[0], axis=0, keepdims=True)
            size = jnp.sum(both[1], axis=0, keepdims=True)
            ratio_d = jnp.sqrt(own) * lax.rsqrt(size + eps)

        step = max(step, 16)

        @pl.loop(0, r2[m].shape[0] // step)
        def _(i):
            rows = pl.ds(pl.multiple_of(i * step, step), step)
            if m < 2:
                own, size = nrm_w[m, 0, rows, :], nrm_w[m, 1, rows, :]
                for n in range(models - 1):
                    own = own + zr_w[m, n, 0, rows, :]
                    size = size + zr_w[m, n, 1, rows, :]
                own = jnp.sum(own, axis=1, keepdims=True)
                size = jnp.sum(size, axis=1, keepdims=True)
                ratio = jnp.sqrt(own) * lax.rsqrt(size + eps)
            else:
                ratio = ratio_d
            new = params[m][rows, :] - learn_rate * (r2[m][rows, :] * ratio)
            r2[m][rows, :] = new
            hb[m][rows, :] = new.astype(bf16)

        copy = pltpu.make_async_copy(r2[m], nexts[m], next_sem.at[m])
        copy.start()
        local.append(copy)
        tall = r2[m].shape[0] // 2
        for h in range(2):
            src = hb[m].at[pl.ds(h * tall, tall)]
            at = piece(m, chip, k, h)
            for way, to in ((1, xn), (2, yn), (0, partner)):
                start(gather(m, h, way, src, at, to))
            copy = pltpu.make_async_copy(src, at, loc_sem.at[m, h])
            copy.start()
            local.append(copy)

    def forward(m):
        at = await_piece(m, 0, 1, chip_x, k)
        start(gather(m, 0, 3, at, at, yn))
        start(gather(m, 0, 4, at, at, partner))
        at = await_piece(m, 1, 2, chip_y, k)
        start(gather(m, 1, 3, at, at, xn))
        start(gather(m, 1, 5, at, at, partner))

    def hand_over(m):
        at = await_piece(m, 1, 1, chip_x, k)
        start(gather(m, 1, 4, at, at, partner))
        at = await_piece(m, 0, 2, chip_y, k)
        start(gather(m, 0, 5, at, at, partner))
        for h in range(2):
            at = await_piece(m, h, 3, chip_d, k)
            start(gather(m, h, 6, at, at, partner))

    steps = len(jobs) // 2
    for t in range(steps + 2):
        for stage, lag in ((stage_1, 0), (stage_2, 1), (stage_3, 2)):
            if 0 <= t - lag < steps:
                for n in (2 * (t - lag), 2 * (t - lag) + 1):
                    stage(n)
        done, rest = divmod(t - 2 + 1, PIECES)
        if t >= 2 and rest == 0 and done >= 1:
            send_sizes(done - 1)
        done, rest = divmod(t - 2, PIECES)
        if t > 2 and rest == 0 and 1 <= done <= 2:
            update(done - 1)
    forward(0)
    update(2)

    for d in range(1, replicas):
        source = lax.rem(me + d, replicas)
        remote(nv_ref, nr.at[source], n_send.at[d - 1], n_recv.at[source], (source, z)).wait_recv()
    tall = hn_ref.shape[0]
    share = nn_ref.shape[0]
    total = nr[0, :tall]
    for n in range(1, replicas):
        total = total + nr[n, :tall]
    for n in range(replicas):
        rows = slice(n * share, (n + 1) * share)
        whole[rows, :] = nr[n, tall : tall + share] - learn_rate * (total[rows] * rate)
    hn_ref[...] = whole[...].astype(bf16)
    nn_ref[...] = whole[pl.ds(me * share, share), :]

    forward(1)
    forward(2)
    for m in range(3):
        hand_over(m)
    for m in range(3):
        for h in range(2):
            await_piece(m, h, 0, chip, 1 - k)
            await_piece(m, h, 4, chip_x, 1 - k)
            await_piece(m, h, 5, chip_y, 1 - k)
            await_piece(m, h, 6, chip_d, 1 - k)
    for copy in local:
        copy.wait()
    for copy in sent:
        copy.wait_send()


def fused(replicas, models):
    def run(
        slope_gate, slope_up, slope_down, slope_norm, param_gate, param_up, param_down, param_norm
    ):
        rows, columns = param_gate.shape
        tall, side = param_down.shape
        units = 2 * PIECES
        tall_n, share = slope_norm.shape[1] // 128, param_norm.shape[0] // 128
        pad = -(tall_n + share) % 8
        vectors = jnp.concatenate(
            [
                slope_norm.reshape(tall_n, 128),
                param_norm.reshape(share, 128),
                jnp.zeros((pad, 128), f32),
            ]
        )
        wide, deep = (rows // units, columns), (tall // units, side)
        V, DMA = pltpu.VMEM, pltpu.SemaphoreType.DMA
        by_chip = (2, replicas // 4, 2, rows, columns)
        shape = jax.ShapeDtypeStruct
        out = pl.pallas_call(
            functools.partial(kernel, replicas, models),
            out_shape=(
                shape((rows * replicas, columns), bf16),
                shape((rows * replicas, columns), bf16),
                shape((tall, side * replicas), bf16),
                shape((rows, columns), f32),
                shape((rows, columns), f32),
                shape((tall, side), f32),
                shape((tall_n, 128), bf16),
                shape((share, 128), f32),
            ),
            in_specs=[pl.BlockSpec(memory_space=pl.ANY)] * 3
            + [pl.BlockSpec(memory_space=pltpu.VMEM)] * 4,
            out_specs=tuple(
                [pl.BlockSpec(memory_space=pl.ANY)] * 6
                + [pl.BlockSpec(memory_space=pltpu.VMEM)] * 2
            ),
            scratch_shapes=[
                V((units, 2, 2) + wide, f32), V((units, 2, 2) + wide, f32), V((units, 2, 2) + deep, f32),
                V((units, 2) + wide, f32), V((units, 2) + wide, f32), V((units, 2) + deep, f32),
                V((rows, columns), f32), V((rows, columns), f32), V((tall, side), f32),
                V((SLOTS, 2, 2) + wide, f32), V((SLOTS, 2, 2) + deep, f32),
                V((rows, columns), bf16), V((rows, columns), bf16), V((tall, side), bf16),
                V((2, 2, rows, 128), f32), V((2, 8, side), f32),
                V((2, models - 1, 2, rows, 128), f32), V((models - 1, 2, 8, side), f32),
                V((replicas,) + vectors.shape, f32), V((tall_n, 128), f32),
                DMA((3, units, 4)), DMA((3, units, 4)), DMA((3, units, 4)),
                DMA((3, units)), DMA((3, units)), DMA((3, units)), DMA((3, units)),
                DMA((3, models - 1)), DMA((3, models - 1)),
                DMA((replicas - 1,)), DMA((replicas,)),
                DMA((3, 2, 7)), DMA((3, 2, 7)), DMA((3, 2)), DMA((3,)),
            ],
            compiler_params=pltpu.CompilerParams(
                collective_id=0, has_side_effects=True, vmem_limit_bytes=67043328
            ),
        )(
            slope_gate.reshape(by_chip), slope_up.reshape(by_chip), slope_down[0],
            vectors, param_gate, param_up, param_down,
        )
        half_gate, half_up, half_down, next_gate, next_up, next_down, half_norm, next_norm = out
        return (
            half_gate, half_up, half_down, half_norm.reshape(-1),
            next_gate, next_up, next_down, next_norm.reshape(-1),
        )

    return run


def plain(
    slope_gate, slope_up, slope_down, slope_norm, param_gate, param_up, param_down, param_norm
):
    rate = lax.axis_size("replica") ** (-0.5)
    halves, nexts = [], []
    for slope, param, dim in (
        (slope_gate, param_gate, 0), (slope_up, param_up, 0), (slope_down, param_down, 1)
    ):
        mean = lax.psum_scatter(slope[0], "replica", scatter_dimension=dim, tiled=True) * rate
        own, size = lax.psum(
            (
                jnp.sum(param * param, axis=1 - dim, keepdims=True),
                jnp.sum(mean * mean, axis=1 - dim, keepdims=True),
            ),
            "model",
        )
        new = param - learn_rate * (mean * (jnp.sqrt(own) * lax.rsqrt(size + eps)))
        nexts.append(new)
        halves.append(lax.all_gather(new.astype(bf16), "replica", axis=dim, tiled=True))
    mean = lax.psum_scatter(slope_norm[0], "replica", scatter_dimension=0, tiled=True) * rate
    new = param_norm - learn_rate * mean
    nexts.append(new)
    halves.append(lax.all_gather(new.astype(bf16), "replica", axis=0, tiled=True))
    return (*halves, *nexts)


def solution(mesh):
    replicas, models = mesh.shape["replica"], mesh.shape["model"]
    body = fused(replicas, models) if replicas == 2 * 2 * 2 else plain
    matrix, turned = P("replica", "model"), P("model", "replica")
    return jax.shard_map(
        body,
        mesh=mesh,
        in_specs=(
            P("replica", None, "model"),
            P("replica", None, "model"),
            P("replica", "model", None),
            P("replica", None),
            matrix, matrix, turned, P("replica"),
        ),
        out_specs=(
            P(None, "model"), P(None, "model"), P("model", None), P(),
            matrix, matrix, turned, P("replica"),
        ),
        check_vma=False,
    )
```

profile of v0, /device:TPU:0, one launch (start us, length us, event | category | flops | bytes accessed | tf_op | source)
XLA Modules:
  0.0 269.9 jit_solution(2350671011911266138)
XLA Ops:
  0.6 0.1 pad.2.clone
  0.7 1.4 maximum_maximum_fusion.nv_ref
  2.1 248.8 %shard_map.143 = (bf16[2048,1536]{1,0:T(8,128)(2,1)}, bf16[2048,1536]{1,0:T(8,128)(2,1)}, bf16[1536,2048]{1,0:T(8,128)(2,1)}, f32[256,1536]{1,0:T(8,128)}, f32[2...) custom-call(f32[2,2,2,256,1536]{4,3,2,1,0:T(8,128)} %bitcast.7, ...), custom_call_target="tpu_custom_call" | custom-call | tf_op jit(solution)/shard_map/pallas_call | solution.py:367
  250.9 0.0 copy-start.1
  250.9 6.1 %copy.24 = bf16[2048,1536]{1,0:T(8,128)(2,1)} copy(bf16[2048,1536]{1,0:T(8,128)(2,1)} %get-tuple-element.32) | data formatting | bytes 12582912
  257.0 0.0 copy-done.1
  257.0 0.0 copy-start
  257.0 3.2 %copy.25 = bf16[2048,1536]{1,0:T(8,128)(2,1)} copy(bf16[2048,1536]{1,0:T(8,128)(2,1)S(1)} %copy-done.1) | data formatting | bytes 12582912
  260.2 1.9 copy-done
  262.1 0.0 copy-start.5
  262.1 0.0 copy-start.4
  262.1 0.0 copy-start.3
  262.1 3.2 %copy.26 = bf16[1536,2048]{1,0:T(8,128)(2,1)} copy(bf16[1536,2048]{1,0:T(8,128)(2,1)S(1)} %copy-done) | data formatting | bytes 12582912
  265.3 0.0 copy-done.5
  265.3 0.0 copy-start.2
  265.3 0.0 copy-start.6
  265.3 0.6 copy.27
  265.9 0.0 copy-done.4
  265.9 1.1 copy.28
  267.0 0.0 copy-done.3
  267.0 1.1 copy.29
  268.2 0.0 copy-done.2
  268.2 1.1 copy.30
  269.3 0.0 copy-done.6
  269.3 0.6 copy.31
  (1 shorter events, 0.0 us)
Async XLA Ops:
  250.9 6.1 %copy-start.1 = (bf16[2048,1536]{1,0:T(8,128)(2,1)S(1)}, bf16[2048,1536]{1,0:T(8,128)(2,1)}, u32[]{:S(2)}) copy-start(bf16[2048,1536]{1,0:T(8,128)(2,1)} %get-tuple-element.33) | copy-start | bytes 18874372
  257.0 5.1 %copy-start = (bf16[1536,2048]{1,0:T(8,128)(2,1)S(1)}, bf16[1536,2048]{1,0:T(8,128)(2,1)}, u32[]{:S(2)}) copy-start(bf16[1536,2048]{1,0:T(8,128)(2,1)} %get-tuple-element.34) | copy-start | bytes 18874372
  262.1 3.2 %copy-start.5 = (bf16[16,128]{1,0:T(8,128)(2,1)S(1)}, bf16[16,128]{1,0:T(8,128)(2,1)}, u32[]{:S(2)}) copy-start(bf16[16,128]{1,0:T(8,128)(2,1)} %get-tuple-element.19) | copy-start | bytes 12292
  262.1 3.8 %copy-start.4 = (f32[256,1536]{1,0:T(8,128)S(1)}, f32[256,1536]{1,0:T(8,128)}, u32[]{:S(2)}) copy-start(f32[256,1536]{1,0:T(8,128)} %get-tuple-element.36) | copy-start | bytes 4718596
  262.1 4.9 %copy-start.3 = (f32[256,1536]{1,0:T(8,128)S(1)}, f32[256,1536]{1,0:T(8,128)}, u32[]{:S(2)}) copy-start(f32[256,1536]{1,0:T(8,128)} %get-tuple-element.37) | copy-start | bytes 4718596
  265.3 2.9 %copy-start.2 = (f32[1536,256]{1,0:T(8,128)S(1)}, f32[1536,256]{1,0:T(8,128)}, u32[]{:S(2)}) copy-start(f32[1536,256]{1,0:T(8,128)} %get-tuple-element.38) | copy-start | bytes 4718596
  265.3 4.0 %copy-start.6 = (f32[2,128]{1,0:T(2,128)S(1)}, f32[2,128]{1,0:T(2,128)}, u32[]{:S(2)}) copy-start(f32[2,128]{1,0:T(2,128)} %get-tuple-element.23) | copy-start | bytes 3076
where the time goes:
time: 270 us
  Pallas kernels  249 us (92%)
  local copies, waits for them, and re-layouts  19 us (7%)
    pallas_call x1, Pallas kernels, run(): pl.pallas_call(functools.partial(kernel, replicas, models), out_shape=(sh...  249 us
    unnamed x22, local copies, waits for them, and re-layouts  18.9 us

commit v1 on v0

--- a/solution.py
+++ b/solution.py
@@ -13,19 +13,77 @@
 f32, bf16 = jnp.float32, jnp.bfloat16
 PIECES = 2
 SLOTS = 4
-
-
-def tile_rows(columns, most=12288):
-    return 8 * max(1, most // (8 * columns))
+OCTAVES = 252.0
+LOW = -125.0
+LN2 = 0.6931471805599453
+
+
+def tile_rows(columns, most=24576):
+    return 16 * max(1, most // (16 * columns))
+
+
+def tiles(shape):
+    return [
+        (slice(r, r + 16), slice(c, c + 128))
+        for r in range(0, shape[0], 16)
+        for c in range(0, shape[1], 128)
+    ]
+
+
+def largest(t):
+    top = None
+    for r in range(0, t.shape[0], 8):
+        for c in range(0, t.shape[1], 128):
+            part = jnp.abs(t[r : r + 8, c : c + 128])
+            top = part if top is None else jnp.maximum(top, part)
+    return top
+
+
+def doubled(t):
+    return jnp.concatenate([t, t], axis=0)
+
+
+def encode(t, scale):
+    power = jnp.exp2(jnp.abs(t) * scale + LOW)
+    return jnp.where(t < 0, -power, power).astype(bf16)
+
+
+def decode(t, slope, base):
+    t = t.astype(f32)
+    size = jnp.log(jnp.abs(t)) * slope + base
+    return jnp.where(t < 0, -size, size)
+
+
+def encoder(top):
+    return doubled(OCTAVES / top)
+
+
+def decoder(top):
+    return doubled(top * (1.0 / (OCTAVES * LN2))), doubled(top * (-LOW / OCTAVES))
+
+
+def decode_block(ref, start, shape, code):
+    rows = []
+    for r in range(0, shape[0], 16):
+        at = pl.ds(pl.multiple_of(start + r, 16), 16)
+        rows.append(
+            jnp.concatenate(
+                [decode(ref[at, c : c + 128], *code) for c in range(0, shape[1], 128)], axis=1
+            )
+        )
+    return jnp.concatenate(rows, axis=0) if len(rows) > 1 else rows[0]
 
 
 def kernel(
     replicas, models,
     g_ref, u_ref, d_ref, nv_ref, pg_ref, pu_ref, pd_ref,
     hg_ref, hu_ref, hd_ref, ng_ref, nu_ref, nd_ref, hn_ref, nn_ref,
-    pr_g, pr_u, pr_d, r1_g, r1_u, r1_d, r2_g, r2_u, r2_d,
-    ow_w, ow_d, hb_g, hb_u, hb_d, nrm_w, nrm_d, zr_w, zr_d, nr, whole,
+    pr_g, pr_u, pr_d, c1_g, c1_u, c1_d, r1_g, r1_u, r1_d,
+    c2_g, c2_u, c2_d, r2_g, r2_u, r2_d, mn_g, mn_u, mn_d,
+    ow_w, ow_d, hb_g, hb_u, hb_d, top1, got1, top2, got2,
+    nrm_w, nrm_d, zs, zr_w, zr_d, ratios, nr, whole,
     ow_sem, pr_send, pr_recv, s1_send, s1_recv, s2_send, s2_recv,
+    t1_send, t1_recv, t2_send, t2_recv,
     z_send, z_recv, n_send, n_recv, ag_send, ag_recv, loc_sem, next_sem,
 ):
     me = lax.axis_index("replica")
@@ -42,10 +100,13 @@
     params = (pg_ref, pu_ref, pd_ref)
     halves = (hg_ref, hu_ref, hd_ref)
     nexts = (ng_ref, nu_ref, nd_ref)
-    pr, r1, r2 = (pr_g, pr_u, pr_d), (r1_g, r1_u, r1_d), (r2_g, r2_u, r2_d)
+    pr, mn = (pr_g, pr_u, pr_d), (mn_g, mn_u, mn_d)
+    c1, r1 = (c1_g, c1_u, c1_d), (r1_g, r1_u, r1_d)
+    c2, r2 = (c2_g, c2_u, c2_d), (r2_g, r2_u, r2_d)
     hb = (hb_g, hb_u, hb_d)
     units = 2 * PIECES
     side = pd_ref.shape[1]
+    bands = pg_ref.shape[0] // 128
 
     others = [lax.rem(me + d, replicas) for d in range(1, replicas)]
     layers = [lax.rem(z + d, models) for d in range(1, models)]
@@ -69,7 +130,7 @@
         sent.append(copy)
 
     def height(m):
-        return r2[m].shape[0] // units
+        return mn[m].shape[0] // units
 
     def views(m, u, core):
         rows = pl.ds(u * height(m), height(m))
@@ -117,20 +178,40 @@
     for n, other in enumerate(others):
         start(remote(nv_ref, nr.at[me], n_send.at[n], n_recv.at[me], (other, z)))
 
-    def first_copy(m, u):
-        if u < PIECES:
-            src, to = pr[m].at[u, :, 1 - x], xn
-        else:
-            src, to = pr[m].at[u, 1 - y], yn
-        return remote(src, r1[m].at[u], s1_send.at[m, u], s1_recv.at[m, u], (to, z))
-
-    def second_copy(m, u):
-        if u < PIECES:
-            src, to = r1[m].at[u, 1 - y], yn
-        else:
-            src, to = r1[m].at[u, 1 - x], xn
-        rows = pl.ds(u * height(m), height(m))
-        return remote(src, r2[m].at[rows], s2_send.at[m, u], s2_recv.at[m, u], (to, z))
+    def first_copies(m, u):
+        to = (xn if u < PIECES else yn, z)
+        return [
+            remote(top1.at[m, u], got1.at[m, u], t1_send.at[m, u], t1_recv.at[m, u], to),
+            remote(c1[m].at[u], r1[m].at[u], s1_send.at[m, u], s1_recv.at[m, u], to),
+        ]
+
+    def second_copies(m, u):
+        to = (yn if u < PIECES else xn, z)
+        return [
+            remote(top2.at[m, u], got2.at[m, u], t2_send.at[m, u], t2_recv.at[m, u], to),
+            remote(c2[m].at[u], r2[m].at[u], s2_send.at[m, u], s2_recv.at[m, u], to),
+        ]
+
+    def sweep(m, body, carry=None):
+        step = tile_rows(mn[m].shape[1])
+        trips = height(m) // step
+        if carry is None:
+            pl.loop(0, trips)(lambda i: body(i * step, step))
+            return None
+        return lax.fori_loop(0, trips, lambda i, c: body(i * step, step, c), carry)
+
+    def code_out(m, values, dst, top):
+        scale = encoder(top)
+
+        def body(at, step):
+            for r in range(0, step, 16):
+                rows = pl.ds(pl.multiple_of(at + r, 16), 16)
+                for c in range(0, mn[m].shape[1], 128):
+                    dst[rows, c : c + 128] = encode(values[rows, c : c + 128], scale)
+
+        sweep(m, body)
+
+    blank = jnp.full((8, 128), 1e-30, f32)
 
     def stage_1(n):
         m, u = jobs[n]
@@ -140,33 +221,54 @@
             copy.wait()
         for copy in pair_copies(m, u):
             copy.wait_recv()
-        step = tile_rows(r2[m].shape[1])
-
-        @pl.loop(0, height(m) // step)
-        def _(i):
-            rows = pl.ds(pl.multiple_of(i * step, step), step)
-            for a in range(2):
-                for b in range(2):
-                    pr[m][u, a, b, rows, :] = pr[m][u, a, b, rows, :] + ow[slot, a, b, rows, :]
-
-        start(first_copy(m, u))
+
+        def add(at, step, a, b):
+            rows = pl.ds(pl.multiple_of(at, 16), step)
+            both = pr[m][u, a, b, rows, :] + ow[slot, a, b, rows, :]
+            pr[m][u, a, b, rows, :] = both
+            return both
+
+        for j in range(2):
+            a, b = (j, 1 - x) if u < PIECES else (1 - y, j)
+            top = sweep(
+                m, lambda at, step, c: jnp.maximum(c, largest(add(at, step, a, b))), blank
+            )
+            top1[m, u, j] = top
+            code_out(m, pr[m].at[u, a, b], c1[m].at[u, j], top)
+        for copy in first_copies(m, u):
+            start(copy)
+        for j in range(2):
+            a, b = (j, x) if u < PIECES else (y, j)
+
+            def keep(at, step):
+                add(at, step, a, b)
+
+            sweep(m, keep)
         if n + SLOTS < len(jobs):
             for copy in own_copies(*jobs[n + SLOTS]):
                 copy.start()
 
     def stage_2(n):
         m, u = jobs[n]
-        first_copy(m, u).wait_recv()
-        step = tile_rows(r2[m].shape[1])
-
-        @pl.loop(0, height(m) // step)
-        def _(i):
-            rows = pl.ds(pl.multiple_of(i * step, step), step)
-            for a in range(2):
-                kept = pr[m][u, a, x, rows, :] if u < PIECES else pr[m][u, y, a, rows, :]
-                r1[m][u, a, rows, :] = r1[m][u, a, rows, :] + kept
-
-        start(second_copy(m, u))
+        for copy in first_copies(m, u):
+            copy.wait_recv()
+        j, a, b = (1 - y, 1 - y, x) if u < PIECES else (1 - x, y, 1 - x)
+        code = decoder(got1[m, u, j])
+        columns = mn[m].shape[1]
+
+        def body(at, step, c):
+            rows = pl.ds(pl.multiple_of(at, 16), step)
+            both = pr[m][u, a, b, rows, :] + decode_block(
+                r1[m].at[u, j], at, (step, columns), code
+            )
+            pr[m][u, a, b, rows, :] = both
+            return jnp.maximum(c, largest(both))
+
+        top = sweep(m, body, blank)
+        top2[m, u] = top
+        code_out(m, pr[m].at[u, a, b], c2[m].at[u], top)
+        for copy in second_copies(m, u):
+            start(copy)
 
     def lanes(t):
         total = t[:, :128]
@@ -182,19 +284,22 @@
 
     def stage_3(n):
         m, u = jobs[n]
-        second_copy(m, u).wait_recv()
-        step = tile_rows(r2[m].shape[1])
-        kept = y if u < PIECES else x
+        for copy in second_copies(m, u):
+            copy.wait_recv()
+        columns = mn[m].shape[1]
+        near = decoder(got1[m, u, y if u < PIECES else x])
+        far = decoder(got2[m, u])
         if m == 2 and u == sequence[0]:
             nrm_d[...] = jnp.zeros_like(nrm_d)
 
-        @pl.loop(0, height(m) // step)
-        def _(i):
-            rows = pl.ds(pl.multiple_of(i * step, step), step)
-            here = pl.ds(pl.multiple_of(u * height(m) + i * step, step), step)
-            mean = (r2[m][here, :] + r1[m][u, kept, rows, :]) * rate
+        def body(at, step):
+            rows = pl.ds(pl.multiple_of(at, 16), step)
+            here = pl.ds(pl.multiple_of(u * height(m) + at, 16), step)
+            kept = r1[m].at[u, y if u < PIECES else x]
+            mean = pr[m][u, y, x, rows, :] + decode_block(kept, at, (step, columns), near)
+            mean = (mean + decode_block(r2[m].at[u], at, (step, columns), far)) * rate
             param = params[m][here, :]
-            r2[m][here, :] = mean
+            mn[m][here, :] = mean
             if m < 2:
                 nrm_w[m, 0, here, :] = lanes(param * param)
                 nrm_w[m, 1, here, :] = lanes(mean * mean)
@@ -202,8 +307,10 @@
                 nrm_d[0] = nrm_d[0] + sublanes(param * param)
                 nrm_d[1] = nrm_d[1] + sublanes(mean * mean)
 
+        sweep(m, body)
+
     def size_copies(m):
-        src = nrm_w.at[m] if m < 2 else nrm_d
+        src = zs.at[m] if m < 2 else nrm_d
         return [
             remote(
                 src, zr_w.at[m, n] if m < 2 else zr_d.at[n],
@@ -213,16 +320,21 @@
         ]
 
     def send_sizes(m):
+        if m < 2:
+            for q in range(2):
+                for b in range(bands):
+                    block = nrm_w[m, q, b * 128 : (b + 1) * 128, :]
+                    row = q * bands + b
+                    zs[m, row : row + 1, :] = jnp.sum(block.T, axis=0, keepdims=True)
         for copy in size_copies(m):
             start(copy)
 
     def piece(m, chip, core, h):
         ref = halves[m]
-        at = pl.multiple_of((2 * chip + core) * r2[0].shape[0], r2[0].shape[0])
+        tall = mn[m].shape[0] // 2
         if m < 2:
-            tall = r2[m].shape[0] // 2
+            at = pl.multiple_of((2 * chip + core) * mn[0].shape[0], mn[0].shape[0])
             return ref.at[pl.ds(pl.multiple_of(at + h * tall, tall), tall), :]
-        tall = r2[m].shape[0] // 2
         at = pl.multiple_of((2 * chip + core) * side, side)
         return ref.at[pl.ds(h * tall, tall), pl.ds(at, side)]
 
@@ -241,7 +353,6 @@
     def update(m):
         for copy in size_copies(m):
             copy.wait_recv()
-        step = tile_rows(r2[m].shape[1])
         if m == 2:
             both = nrm_d[...]
             for n in range(models - 1):
@@ -249,31 +360,31 @@
             own = jnp.sum(both[0], axis=0, keepdims=True)
             size = jnp.sum(both[1], axis=0, keepdims=True)
             ratio_d = jnp.sqrt(own) * lax.rsqrt(size + eps)
-
-        step = max(step, 16)
-
-        @pl.loop(0, r2[m].shape[0] // step)
-        def _(i):
-            rows = pl.ds(pl.multiple_of(i * step, step), step)
-            if m < 2:
-                own, size = nrm_w[m, 0, rows, :], nrm_w[m, 1, rows, :]
-                for n in range(models - 1):
-                    own = own + zr_w[m, n, 0, rows, :]
-                    size = size + zr_w[m, n, 1, rows, :]
-                own = jnp.sum(own, axis=1, keepdims=True)
-                size = jnp.sum(size, axis=1, keepdims=True)
-                ratio = jnp.sqrt(own) * lax.rsqrt(size + eps)
-            else:
-                ratio = ratio_d
-            new = params[m][rows, :] - learn_rate * (r2[m][rows, :] * ratio)
-            r2[m][rows, :] = new
-            hb[m][rows, :] = new.astype(bf16)
-
-        copy = pltpu.make_async_copy(r2[m], nexts[m], next_sem.at[m])
-        copy.start()
-        local.append(copy)
-        tall = r2[m].shape[0] // 2
+        else:
+            both = zs[m]
+            for n in range(models - 1):
+                both = both + zr_w[m, n]
+            ratio = jnp.sqrt(both[:bands]) * lax.rsqrt(both[bands : 2 * bands] + eps)
+            for b in range(bands):
+                ratios[b * 128 : (b + 1) * 128, :] = jnp.broadcast_to(
+                    ratio[b : b + 1], (128, 128)
+                ).T
+        columns = mn[m].shape[1]
+        step = tile_rows(columns)
+        tall = mn[m].shape[0] // 2
         for h in range(2):
+
+            @pl.loop(0, tall // step)
+            def _(i):
+                rows = pl.ds(pl.multiple_of(h * tall + i * step, 16), step)
+                if m < 2:
+                    ratio = jnp.concatenate([ratios[rows, :]] * (columns // 128), axis=1)
+                else:
+                    ratio = ratio_d
+                new = params[m][rows, :] - learn_rate * (mn[m][rows, :] * ratio)
+                mn[m][rows, :] = new
+                hb[m][rows, :] = new.astype(bf16)
+
             src = hb[m].at[pl.ds(h * tall, tall)]
             at = piece(m, chip, k, h)
             for way, to in ((1, xn), (2, yn), (0, partner)):
@@ -281,6 +392,9 @@
             copy = pltpu.make_async_copy(src, at, loc_sem.at[m, h])
             copy.start()
             local.append(copy)
+        copy = pltpu.make_async_copy(mn[m], nexts[m], next_sem.at[m])
+        copy.start()
+        local.append(copy)
 
     def forward(m):
         at = await_piece(m, 0, 1, chip_x, k)
@@ -364,6 +478,10 @@
         V, DMA = pltpu.VMEM, pltpu.SemaphoreType.DMA
         by_chip = (2, replicas // 4, 2, rows, columns)
         shape = jax.ShapeDtypeStruct
+
+        def three(front, dtype):
+            return [V(front + wide, dtype), V(front + wide, dtype), V(front + deep, dtype)]
+
         out = pl.pallas_call(
             functools.partial(kernel, replicas, models),
             out_shape=(
@@ -383,15 +501,19 @@
                 + [pl.BlockSpec(memory_space=pltpu.VMEM)] * 2
             ),
             scratch_shapes=[
-                V((units, 2, 2) + wide, f32), V((units, 2, 2) + wide, f32), V((units, 2, 2) + deep, f32),
-                V((units, 2) + wide, f32), V((units, 2) + wide, f32), V((units, 2) + deep, f32),
+                *three((units, 2, 2), f32), *three((units, 2), bf16), *three((units, 2), bf16),
+                *three((units,), bf16), *three((units,), bf16),
                 V((rows, columns), f32), V((rows, columns), f32), V((tall, side), f32),
                 V((SLOTS, 2, 2) + wide, f32), V((SLOTS, 2, 2) + deep, f32),
                 V((rows, columns), bf16), V((rows, columns), bf16), V((tall, side), bf16),
+                V((3, units, 2, 8, 128), f32), V((3, units, 2, 8, 128), f32),
+                V((3, units, 8, 128), f32), V((3, units, 8, 128), f32),
                 V((2, 2, rows, 128), f32), V((2, 8, side), f32),
-                V((2, models - 1, 2, rows, 128), f32), V((models - 1, 2, 8, side), f32),
+                V((2, 2 * rows // 128, 128), f32), V((2, models - 1, 2 * rows // 128, 128), f32),
+                V((models - 1, 2, 8, side), f32), V((rows, 128), f32),
                 V((replicas,) + vectors.shape, f32), V((tall_n, 128), f32),
                 DMA((3, units, 4)), DMA((3, units, 4)), DMA((3, units, 4)),
+                DMA((3, units)), DMA((3, units)), DMA((3, units)), DMA((3, units)),
                 DMA((3, units)), DMA((3, units)), DMA((3, units)), DMA((3, units)),
                 DMA((3, models - 1)), DMA((3, models - 1)),
                 DMA((replicas - 1,)), DMA((replicas,)),

time: 270 us -> 197 us (0.73)
  Pallas kernels: 249 us -> 175 us
    pallas_call x1, Pallas kernels: 249 us -> 175 us  [run(): pl.pallas_call(functools.partial(kernel, replicas, models), out_shape=(sh...]
where the time goes in v1:
time: 197 us; the launch traced here: 196 us
  Pallas kernels  175 us (89%)
  local copies, waits for them, and re-layouts  19 us (10%)
    pallas_call x1, Pallas kernels, run(): pl.pallas_call(functools.partial(kernel, replicas, models), out_shape=(sh...  175 us
    unnamed x22, local copies, waits for them, and re-layouts  18.9 us

profile of v1, /device:TPU:0, one launch (start us, length us, event | category | flops | bytes accessed | tf_op | source)
XLA Modules:
  0.0 196.3 jit_solution(2100314875731631213)
XLA Ops:
  0.6 0.1 pad.2.clone
  0.7 1.4 maximum_maximum_fusion.nv_ref
  2.1 175.3 %shard_map.143 = (bf16[2048,1536]{1,0:T(8,128)(2,1)}, bf16[2048,1536]{1,0:T(8,128)(2,1)}, bf16[1536,2048]{1,0:T(8,128)(2,1)}, f32[256,1536]{1,0:T(8,128)}, f32[2...) custom-call(f32[2,2,2,256,1536]{4,3,2,1,0:T(8,128)} %bitcast.7, ...), custom_call_target="tpu_custom_call" | custom-call | tf_op jit(solution)/shard_map/pallas_call | solution.py:485
  177.4 0.0 copy-start.1
  177.4 6.1 %copy.24 = bf16[2048,1536]{1,0:T(8,128)(2,1)} copy(bf16[2048,1536]{1,0:T(8,128)(2,1)} %get-tuple-element.32) | data formatting | bytes 12582912
  183.4 0.0 copy-done.1
  183.4 0.0 copy-start
  183.5 3.2 %copy.25 = bf16[2048,1536]{1,0:T(8,128)(2,1)} copy(bf16[2048,1536]{1,0:T(8,128)(2,1)S(1)} %copy-done.1) | data formatting | bytes 12582912
  186.6 1.9 copy-done
  188.5 0.0 copy-start.5
  188.5 0.0 copy-start.4
  188.5 0.0 copy-start.3
  188.5 3.2 %copy.26 = bf16[1536,2048]{1,0:T(8,128)(2,1)} copy(bf16[1536,2048]{1,0:T(8,128)(2,1)S(1)} %copy-done) | data formatting | bytes 12582912
  191.7 0.0 copy-done.5
  191.7 0.0 copy-start.2
  191.7 0.0 copy-start.6
  191.7 0.6 copy.27
  192.3 0.0 copy-done.4
  192.3 1.1 copy.28
  193.5 0.0 copy-done.3
  193.5 1.1 copy.29
  194.6 0.0 copy-done.2
  194.6 1.1 copy.30
  195.7 0.0 copy-done.6
  195.7 0.6 copy.31
  (1 shorter events, 0.0 us)
Async XLA Ops:
  177.4 6.1 %copy-start.1 = (bf16[2048,1536]{1,0:T(8,128)(2,1)S(1)}, bf16[2048,1536]{1,0:T(8,128)(2,1)}, u32[]{:S(2)}) copy-start(bf16[2048,1536]{1,0:T(8,128)(2,1)} %get-tuple-element.33) | copy-start | bytes 18874372
  183.4 5.1 %copy-start = (bf16[1536,2048]{1,0:T(8,128)(2,1)S(1)}, bf16[1536,2048]{1,0:T(8,128)(2,1)}, u32[]{:S(2)}) copy-start(bf16[1536,2048]{1,0:T(8,128)(2,1)} %get-tuple-element.34) | copy-start | bytes 18874372
  188.5 3.2 %copy-start.5 = (bf16[16,128]{1,0:T(8,128)(2,1)S(1)}, bf16[16,128]{1,0:T(8,128)(2,1)}, u32[]{:S(2)}) copy-start(bf16[16,128]{1,0:T(8,128)(2,1)} %get-tuple-element.19) | copy-start | bytes 12292
  188.5 3.8 %copy-start.4 = (f32[256,1536]{1,0:T(8,128)S(1)}, f32[256,1536]{1,0:T(8,128)}, u32[]{:S(2)}) copy-start(f32[256,1536]{1,0:T(8,128)} %get-tuple-element.36) | copy-start | bytes 4718596
  188.5 4.9 %copy-start.3 = (f32[256,1536]{1,0:T(8,128)S(1)}, f32[256,1536]{1,0:T(8,128)}, u32[]{:S(2)}) copy-start(f32[256,1536]{1,0:T(8,128)} %get-tuple-element.37) | copy-start | bytes 4718596
  191.7 2.9 %copy-start.2 = (f32[1536,256]{1,0:T(8,128)S(1)}, f32[1536,256]{1,0:T(8,128)}, u32[]{:S(2)}) copy-start(f32[1536,256]{1,0:T(8,128)} %get-tuple-element.38) | copy-start | bytes 4718596
  191.7 4.0 %copy-start.6 = (f32[2,128]{1,0:T(2,128)S(1)}, f32[2,128]{1,0:T(2,128)}, u32[]{:S(2)}) copy-start(f32[2,128]{1,0:T(2,128)} %get-tuple-element.23) | copy-start | bytes 3076

commit v2 on v1

v2 whole, which is shorter than its diff:
```python
import functools

import jax
import jax.numpy as jnp
from jax import lax
from jax.experimental import pallas as pl
from jax.experimental.pallas import tpu as pltpu
from jax.sharding import PartitionSpec as P

learn_rate = 0.5
eps = 1e-06
MESH = pl.DeviceIdType.MESH
f32, bf16 = jnp.float32, jnp.bfloat16
PIECES = 2
SLOTS = 2
KERNEL_BYTES = 43000000
OCTAVES = 252.0
LOW = -125.0
LN2 = 0.6931471805599453


def tile_rows(columns, most=24576):
    return 16 * max(1, most // (16 * columns))


def tiles(shape):
    return [
        (slice(r, r + 16), slice(c, c + 128))
        for r in range(0, shape[0], 16)
        for c in range(0, shape[1], 128)
    ]


def largest(t):
    top = None
    for r in range(0, t.shape[0], 8):
        for c in range(0, t.shape[1], 128):
            part = jnp.abs(t[r : r + 8, c : c + 128])
            top = part if top is None else jnp.maximum(top, part)
    return top


def doubled(t):
    return jnp.concatenate([t, t], axis=0)


def encode(t, scale):
    power = jnp.exp2(jnp.abs(t) * scale + LOW)
    return jnp.where(t < 0, -power, power).astype(bf16)


def decode(t, slope, base):
    t = t.astype(f32)
    size = jnp.log(jnp.abs(t)) * slope + base
    return jnp.where(t < 0, -size, size)


def encoder(top):
    return doubled(OCTAVES / top)


def decoder(top):
    return doubled(top * (1.0 / (OCTAVES * LN2))), doubled(top * (-LOW / OCTAVES))


def decode_block(ref, start, shape, code):
    rows = []
    for r in range(0, shape[0], 16):
        at = pl.ds(pl.multiple_of(start + r, 16), 16)
        rows.append(
            jnp.concatenate(
                [decode(ref[at, c : c + 128], *code) for c in range(0, shape[1], 128)], axis=1
            )
        )
    return jnp.concatenate(rows, axis=0) if len(rows) > 1 else rows[0]


def settle(copies):
    for copy in copies:
        copy.wait_recv()


def kernel(
    replicas, models,
    g_ref, u_ref, d_ref, pg_ref, pu_ref, pd_ref, sn_ref, pn_ref,
    hg_ref, hu_ref, hd_ref, ng_ref, nu_ref, nd_ref, hn_ref, nn_ref,
    pr_g, pr_u, pr_d, r1_g, r1_u, r1_d, r2_g, r2_u, r2_d, pm_g, pm_u, pm_d,
    c1_w, c1_d, c2_w, c2_d, ow_w, ow_d, top1, got1, top2, got2,
    nrm_w, nrm_d, zs, zr_w, zr_d, ratios, nr, whole,
    ow_sem, pm_sem, pr_send, pr_recv, s1_send, s1_recv, s2_send, s2_recv,
    t1_send, t1_recv, t2_send, t2_recv,
    z_send, z_recv, n_send, n_recv, ag_send, ag_recv,
):
    me = lax.axis_index("replica")
    z = lax.axis_index("model")
    k = lax.rem(me, 2)
    x = lax.rem(me // 2, 2)
    y = me // 4
    partner = me + 1 - 2 * k
    xn = me + 2 - 4 * x
    yn = me + 4 - 8 * y
    rate = replicas ** (-0.5)

    slopes = (g_ref, u_ref, d_ref)
    halves = (hg_ref, hu_ref, hd_ref)
    mn = (ng_ref, nu_ref, nd_ref)
    pr, r1, r2 = (pr_g, pr_u, pr_d), (r1_g, r1_u, r1_d), (r2_g, r2_u, r2_d)
    params = (pm_g, pm_u, pm_d)
    units = 2 * PIECES
    side = nd_ref.shape[1]
    bands = ng_ref.shape[0] // 128

    others = [lax.rem(me + d, replicas) for d in range(1, replicas)]
    layers = [lax.rem(z + d, models) for d in range(1, models)]
    barrier = pltpu.get_barrier_semaphore()
    for other in others:
        pl.semaphore_signal(barrier, inc=1, device_id=(other, z), device_id_type=MESH)
    for layer in layers:
        pl.semaphore_signal(barrier, inc=1, device_id=(me, layer), device_id_type=MESH)

    sequence = [h * PIECES + j for j in range(PIECES) for h in range(2)]
    jobs = [(m, u) for m in range(3) for u in sequence]
    steps = len(jobs) // 2

    def remote(src, dst, send_sem, recv_sem, to):
        return pltpu.make_async_remote_copy(
            src_ref=src, dst_ref=dst, send_sem=send_sem, recv_sem=recv_sem,
            device_id=to, device_id_type=MESH,
        )

    sent = []

    def start(copy):
        copy.start()
        sent.append(copy)

    def height(m):
        return mn[m].shape[0] // units

    def parts(u):
        if u < PIECES:
            return [(1 - y, 1 - x), (y, 1 - x), (1 - y, x), (y, x)]
        return [(1 - y, 1 - x), (1 - y, x), (y, 1 - x), (y, x)]

    def view(m, u, q, core):
        rows = pl.ds(u * height(m), height(m))
        a, b = parts(u)[q]
        if m < 2:
            return slopes[m].at[a, b, core, rows, :]
        at = pl.multiple_of((2 * (2 * a + b) + core) * side, side)
        return slopes[m].at[rows, pl.ds(at, side)]

    def own_copy(n, q):
        m, u = jobs[n]
        ow = ow_w if m < 2 else ow_d
        return pltpu.make_async_copy(view(m, u, q, k), ow.at[n % SLOTS, q], ow_sem.at[m, u, q])

    def pair_copy(n, q):
        m, u = jobs[n]
        return remote(
            view(m, u, q, 1 - k), pr[m].at[u, q],
            pr_send.at[m, u, q], pr_recv.at[m, u, q], (partner, z),
        )

    for n in range(SLOTS):
        for q in range(4):
            own_copy(n, q).start()
    loads = [
        pltpu.make_async_copy(src, params[m], pm_sem.at[m])
        for m, src in enumerate((pg_ref, pu_ref, pd_ref))
    ]

    pl.semaphore_wait(barrier, replicas - 1 + models - 1)

    for q in range(2):
        for n in range(2):
            start(pair_copy(n, q))
    for n in range(2):
        for q in range(2, 4):
            start(pair_copy(n, q))
    for n in range(2, len(jobs)):
        for q in range(4):
            start(pair_copy(n, q))
    for copy in loads:
        copy.start()

    def slot_of(n):
        m = jobs[n][0]
        return (c1_w, c2_w, n % units) if m < 2 else (c1_d, c2_d, n % units)

    def first_copies(n, p):
        m, u = jobs[n]
        to = (xn if u < PIECES else yn, z)
        c1, _, slot = slot_of(n)
        return [
            remote(
                top1.at[m, u, p], got1.at[m, u, p], t1_send.at[m, u, p], t1_recv.at[m, u, p], to
            ),
            remote(
                c1.at[slot, p], r1[m].at[u, p], s1_send.at[m, u, p], s1_recv.at[m, u, p], to
            ),
        ]

    def second_copies(n):
        m, u = jobs[n]
        to = (yn if u < PIECES else xn, z)
        _, c2, slot = slot_of(n)
        return [
            remote(top2.at[m, u], got2.at[m, u], t2_send.at[m, u], t2_recv.at[m, u], to),
            remote(c2.at[slot], r2[m].at[u], s2_send.at[m, u], s2_recv.at[m, u], to),
        ]

    def reused(n):
        return jobs[n][0] == 1

    def sweep(m, body, carry=None):
        step = tile_rows(mn[m].shape[1])
        trips = height(m) // step
        if carry is None:
            pl.loop(0, trips)(lambda i: body(i * step, step))
            return None
        return lax.fori_loop(0, trips, lambda i, c: body(i * step, step, c), carry)

    def code_out(m, values, dst, top):
        scale = encoder(top)

        def body(at, step):
            for r in range(0, step, 16):
                rows = pl.ds(pl.multiple_of(at + r, 16), 16)
                for c in range(0, mn[m].shape[1], 128):
                    dst[rows, c : c + 128] = encode(values[rows, c : c + 128], scale)

        sweep(m, body)

    blank = jnp.full((8, 128), 1e-30, f32)

    def add(n, q, at, step):
        m, u = jobs[n]
        ow = ow_w if m < 2 else ow_d
        rows = pl.ds(pl.multiple_of(at, 16), step)
        both = pr[m][u, q, rows, :] + ow[n % SLOTS, q, rows, :]
        pr[m][u, q, rows, :] = both
        return both

    def stage_1(n, p):
        m, u = jobs[n]
        own_copy(n, p).wait()
        settle([pair_copy(n, p)])
        top = sweep(
            m, lambda at, step, c: jnp.maximum(c, largest(add(n, p, at, step))), blank
        )
        top1[m, u, p] = top
        c1, _, slot = slot_of(n)
        if reused(n):
            for copy in first_copies(n - units, p):
                copy.wait_send()
        code_out(m, pr[m].at[u, p], c1.at[slot, p], top)
        for copy in first_copies(n, p):
            copy.start()

    def stage_1_rest(n):
        m, u = jobs[n]
        for q in range(2, 4):
            own_copy(n, q).wait()
            settle([pair_copy(n, q)])

            def keep(at, step):
                add(n, q, at, step)

            sweep(m, keep)
        if n + SLOTS < len(jobs):
            for q in range(4):
                own_copy(n + SLOTS, q).start()

    def stage_2(n):
        m, u = jobs[n]
        settle(first_copies(n, 0))
        code = decoder(got1[m, u, 0])
        columns = mn[m].shape[1]

        def body(at, step, c):
            rows = pl.ds(pl.multiple_of(at, 16), step)
            both = pr[m][u, 2, rows, :] + decode_block(r1[m].at[u, 0], at, (step, columns), code)
            pr[m][u, 2, rows, :] = both
            return jnp.maximum(c, largest(both))

        top = sweep(m, body, blank)
        top2[m, u] = top
        _, c2, slot = slot_of(n)
        if reused(n):
            for copy in second_copies(n - units):
                copy.wait_send()
        code_out(m, pr[m].at[u, 2], c2.at[slot], top)
        for copy in second_copies(n):
            copy.start()

    def lanes(t):
        total = t[:, :128]
        for c in range(1, t.shape[1] // 128):
            total = total + t[:, c * 128 : (c + 1) * 128]
        return total

    def sublanes(t):
        total = t[:8]
        for c in range(1, t.shape[0] // 8):
            total = total + t[c * 8 : (c + 1) * 8]
        return total

    def stage_3(n):
        m, u = jobs[n]
        settle(first_copies(n, 1))
        settle(second_copies(n))
        columns = mn[m].shape[1]
        near, far = decoder(got1[m, u, 1]), decoder(got2[m, u])
        if u == sequence[0]:
            loads[m].wait()
            if m == 2:
                nrm_d[...] = jnp.zeros_like(nrm_d)

        def body(at, step):
            rows = pl.ds(pl.multiple_of(at, 16), step)
            here = pl.ds(pl.multiple_of(u * height(m) + at, 16), step)
            mean = pr[m][u, 3, rows, :] + decode_block(r1[m].at[u, 1], at, (step, columns), near)
            mean = (mean + decode_block(r2[m].at[u], at, (step, columns), far)) * rate
            param = params[m][here, :]
            mn[m][here, :] = mean
            if m < 2:
                nrm_w[0, here, :] = lanes(param * param)
                nrm_w[1, here, :] = lanes(mean * mean)
            else:
                nrm_d[0] = nrm_d[0] + sublanes(param * param)
                nrm_d[1] = nrm_d[1] + sublanes(mean * mean)

        sweep(m, body)

    def size_copies(m):
        src = zs.at[m] if m < 2 else nrm_d
        return [
            remote(
                src, zr_w.at[m, n] if m < 2 else zr_d.at[n],
                z_send.at[m, n], z_recv.at[m, n], (me, layer),
            )
            for n, layer in enumerate(layers)
        ]

    def send_sizes(m):
        if m < 2:
            for q in range(2):
                for b in range(bands):
                    block = nrm_w[q, b * 128 : (b + 1) * 128, :]
                    row = q * bands + b
                    zs[m, row : row + 1, :] = jnp.sum(block.T, axis=0, keepdims=True)
        for copy in size_copies(m):
            start(copy)

    def piece(m, chip, core, h):
        ref = halves[m]
        tall = mn[m].shape[0] // 2
        if m < 2:
            at = pl.multiple_of((2 * chip + core) * mn[0].shape[0], mn[0].shape[0])
            return ref.at[pl.ds(pl.multiple_of(at + h * tall, tall), tall), :]
        at = pl.multiple_of((2 * chip + core) * side, side)
        return ref.at[pl.ds(h * tall, tall), pl.ds(at, side)]

    chip, chip_x, chip_y, chip_d = me // 2, xn // 2, yn // 2, 3 - me // 2

    def gather(m, h, way, at, to):
        return remote(at, at, ag_send.at[m, h, way], ag_recv.at[m, h, way], (to, z))

    def await_piece(m, h, way, chip_from, core):
        at = piece(m, chip_from, core, h)
        settle([gather(m, h, way, at, partner)])
        return at

    def update(m):
        settle(size_copies(m))
        if m == 2:
            both = nrm_d[...]
            for n in range(models - 1):
                both = both + zr_d[n]
            own = jnp.sum(both[0], axis=0, keepdims=True)
            size = jnp.sum(both[1], axis=0, keepdims=True)
            ratio_d = jnp.sqrt(own) * lax.rsqrt(size + eps)
        else:
            both = zs[m]
            for n in range(models - 1):
                both = both + zr_w[m, n]
            ratio = jnp.sqrt(both[:bands]) * lax.rsqrt(both[bands : 2 * bands] + eps)
            for b in range(bands):
                ratios[b * 128 : (b + 1) * 128, :] = jnp.broadcast_to(
                    ratio[b : b + 1], (128, 128)
                ).T
        columns = mn[m].shape[1]
        step = tile_rows(columns)
        tall = mn[m].shape[0] // 2
        for h in range(2):
            at = piece(m, chip, k, h)

            @pl.loop(0, tall // step)
            def _(i):
                here = pl.ds(pl.multiple_of(i * step, 16), step)
                rows = pl.ds(pl.multiple_of(h * tall + i * step, 16), step)
                if m < 2:
                    ratio = jnp.concatenate([ratios[rows, :]] * (columns // 128), axis=1)
                else:
                    ratio = ratio_d
                new = params[m][rows, :] - learn_rate * (mn[m][rows, :] * ratio)
                mn[m][rows, :] = new
                at[here, :] = new.astype(bf16)

            for way, to in ((1, xn), (2, yn), (0, partner)):
                start(gather(m, h, way, at, to))

    def forward(m):
        at = await_piece(m, 0, 1, chip_x, k)
        start(gather(m, 0, 3, at, yn))
        start(gather(m, 0, 4, at, partner))
        at = await_piece(m, 1, 2, chip_y, k)
        start(gather(m, 1, 3, at, xn))
        start(gather(m, 1, 5, at, partner))

    def hand_over(m):
        at = await_piece(m, 1, 1, chip_x, k)
        start(gather(m, 1, 4, at, partner))
        at = await_piece(m, 0, 2, chip_y, k)
        start(gather(m, 0, 5, at, partner))
        for h in range(2):
            at = await_piece(m, h, 3, chip_d, k)
            start(gather(m, h, 6, at, partner))

    tall, share = hn_ref.shape[0], nn_ref.shape[0]

    def send_vectors():
        nr[me, :tall] = sn_ref[...]
        nr[me, tall:] = jnp.concatenate(
            [pn_ref[...], jnp.zeros((nr.shape[1] - tall - share, 128), f32)]
        )
        for n, other in enumerate(others):
            start(remote(nr.at[me], nr.at[me], n_send.at[n], n_recv.at[me], (other, z)))

    def finish_vectors():
        for d in range(1, replicas):
            source = lax.rem(me + d, replicas)
            at = nr.at[source]
            settle([remote(at, at, n_send.at[d - 1], n_recv.at[source], (source, z))])
        total = nr[0, :tall]
        for n in range(1, replicas):
            total = total + nr[n, :tall]
        for n in range(replicas):
            rows = slice(n * share, (n + 1) * share)
            whole[rows, :] = nr[n, tall : tall + share] - learn_rate * (total[rows] * rate)
        hn_ref[...] = whole[...].astype(bf16)
        nn_ref[...] = whole[pl.ds(me * share, share), :]

    for t in range(steps + 2):
        if t < steps:
            for p in range(2):
                for n in (2 * t, 2 * t + 1):
                    stage_1(n, p)
            for n in (2 * t, 2 * t + 1):
                stage_1_rest(n)
        if t == 0:
            send_vectors()
        for stage, lag in ((stage_2, 1), (stage_3, 2)):
            if 0 <= t - lag < steps:
                for n in (2 * (t - lag), 2 * (t - lag) + 1):
                    stage(n)
        done, rest = divmod(t - 2 + 1, PIECES)
        if t >= 2 and rest == 0 and done >= 1:
            send_sizes(done - 1)
        done, rest = divmod(t - 2, PIECES)
        if t > 2 and rest == 0 and 1 <= done <= 2:
            update(done - 1)
    forward(0)
    update(2)
    finish_vectors()
    forward(1)
    forward(2)
    for m in range(3):
        hand_over(m)
    for m in range(3):
        for h in range(2):
            await_piece(m, h, 0, chip, 1 - k)
            await_piece(m, h, 4, chip_x, 1 - k)
            await_piece(m, h, 5, chip_y, 1 - k)
            await_piece(m, h, 6, chip_d, 1 - k)
    for n in range(len(jobs)):
        if n + units >= len(jobs) or not reused(n + units):
            for copy in first_copies(n, 0) + first_copies(n, 1) + second_copies(n):
                copy.wait_send()
    for copy in sent:
        copy.wait_send()


def put(*refs):
    count = len(refs) // 2
    ins, outs, sem = refs[:count], refs[count : 2 * count], refs[2 * count]
    copies = [
        pltpu.make_async_copy(src, dst, sem.at[n])
        for n, (src, dst) in enumerate(zip(ins, outs))
    ]
    for copy in copies:
        copy.start()
    for copy in copies:
        copy.wait()


def fused(replicas, models):
    def run(
        slope_gate, slope_up, slope_down, slope_norm, param_gate, param_up, param_down, param_norm
    ):
        rows, columns = param_gate.shape
        tall, side = param_down.shape
        units = 2 * PIECES
        tall_n, share = slope_norm.shape[1] // 128, param_norm.shape[0] // 128
        lines = tall_n + share + -(tall_n + share) % 8
        wide, deep = (rows // units, columns), (tall // units, side)
        V, DMA = pltpu.VMEM, pltpu.SemaphoreType.DMA
        by_chip = (2, replicas // 4, 2, rows, columns)
        whole, inside = pl.BlockSpec(memory_space=pl.ANY), pl.BlockSpec(memory_space=pltpu.VMEM)

        def three(front, dtype):
            return [V(front + wide, dtype), V(front + wide, dtype), V(front + deep, dtype)]

        out = pl.pallas_call(
            functools.partial(kernel, replicas, models),
            out_shape=(
                V((rows * replicas, columns), bf16),
                V((rows * replicas, columns), bf16),
                V((tall, side * replicas), bf16),
                V((rows, columns), f32),
                V((rows, columns), f32),
                V((tall, side), f32),
                V((tall_n, 128), bf16),
                V((share, 128), f32),
            ),
            in_specs=[whole] * 6 + [inside] * 2,
            out_specs=tuple([inside] * 8),
            scratch_shapes=[
                *three((units, 4), f32), *three((units, 2), bf16), *three((units,), bf16),
                V((rows, columns), f32), V((rows, columns), f32), V((tall, side), f32),
                V((units, 2) + wide, bf16), V((units, 2) + deep, bf16),
                V((units,) + wide, bf16), V((units,) + deep, bf16),
                V((SLOTS, 4) + wide, f32), V((SLOTS, 4) + deep, f32),
                V((3, units, 2, 8, 128), f32), V((3, units, 2, 8, 128), f32),
                V((3, units, 8, 128), f32), V((3, units, 8, 128), f32),
                V((2, rows, 128), f32), V((2, 8, side), f32),
                V((2, 2 * rows // 128, 128), f32), V((2, models - 1, 2 * rows // 128, 128), f32),
                V((models - 1, 2, 8, side), f32), V((rows, 128), f32),
                V((replicas, lines, 128), f32), V((tall_n, 128), f32),
                DMA((3, units, 4)), DMA((3,)), DMA((3, units, 4)), DMA((3, units, 4)),
                DMA((3, units, 2)), DMA((3, units, 2)), DMA((3, units)), DMA((3, units)),
                DMA((3, units, 2)), DMA((3, units, 2)), DMA((3, units)), DMA((3, units)),
                DMA((3, models - 1)), DMA((3, models - 1)),
                DMA((replicas - 1,)), DMA((replicas,)),
                DMA((3, 2, 7)), DMA((3, 2, 7)),
            ],
            compiler_params=pltpu.CompilerParams(
                collective_id=0, has_side_effects=True, vmem_limit_bytes=KERNEL_BYTES
            ),
        )(
            slope_gate.reshape(by_chip), slope_up.reshape(by_chip), slope_down[0],
            param_gate, param_up, param_down,
            slope_norm.reshape(tall_n, 128), param_norm.reshape(share, 128),
        )
        half_gate, half_up, half_down, next_gate, next_up, next_down, half_norm, next_norm = (
            pl.pallas_call(
                put,
                out_shape=tuple(jax.ShapeDtypeStruct(o.shape, o.dtype) for o in out),
                in_specs=[inside] * len(out),
                out_specs=tuple([whole] * len(out)),
                scratch_shapes=[DMA((len(out),))],
                compiler_params=pltpu.CompilerParams(vmem_limit_bytes=1 << 20),
            )(*[pltpu.with_memory_space_constraint(o, pltpu.VMEM) for o in out])
        )
        return (
            half_gate, half_up, half_down, half_norm.reshape(-1),
            next_gate, next_up, next_down, next_norm.reshape(-1),
        )

    return run


def plain(
    slope_gate, slope_up, slope_down, slope_norm, param_gate, param_up, param_down, param_norm
):
    rate = lax.axis_size("replica") ** (-0.5)
    halves, nexts = [], []
    for slope, param, dim in (
        (slope_gate, param_gate, 0), (slope_up, param_up, 0), (slope_down, param_down, 1)
    ):
        mean = lax.psum_scatter(slope[0], "replica", scatter_dimension=dim, tiled=True) * rate
        own, size = lax.psum(
            (
                jnp.sum(param * param, axis=1 - dim, keepdims=True),
                jnp.sum(mean * mean, axis=1 - dim, keepdims=True),
            ),
            "model",
        )
        new = param - learn_rate * (mean * (jnp.sqrt(own) * lax.rsqrt(size + eps)))
        nexts.append(new)
        halves.append(lax.all_gather(new.astype(bf16), "replica", axis=dim, tiled=True))
    mean = lax.psum_scatter(slope_norm[0], "replica", scatter_dimension=0, tiled=True) * rate
    new = param_norm - learn_rate * mean
    nexts.append(new)
    halves.append(lax.all_gather(new.astype(bf16), "replica", axis=0, tiled=True))
    return (*halves, *nexts)


def solution(mesh):
    replicas, models = mesh.shape["replica"], mesh.shape["model"]
    body = fused(replicas, models) if replicas == 2 * 2 * 2 else plain
    matrix, turned = P("replica", "model"), P("model", "replica")
    return jax.shard_map(
        body,
        mesh=mesh,
        in_specs=(
            P("replica", None, "model"),
            P("replica", None, "model"),
            P("replica", "model", None),
            P("replica", None),
            matrix, matrix, turned, P("replica"),
        ),
        out_specs=(
            P(None, "model"), P(None, "model"), P("model", None), P(),
            matrix, matrix, turned, P("replica"),
        ),
        check_vma=False,
    )
```

time: 197 us -> 179 us (0.909)
  local copies, waits for them, and re-layouts: 19 us -> 0 us
  Pallas kernels: 175 us -> 178 us
    unnamed x22 -> x0, local copies, waits for them, and re-layouts: 18.9 us -> none
    pallas_call x1 -> x2, Pallas kernels: 175 us -> 178 us  [the longest x1 170 us: run(): pl.pallas_call(functools.partial(kernel, replicas, models), out_shape=(V(...]
where the time goes in v2:
time: 179 us
  Pallas kernels  178 us (99%)
    pallas_call x1, Pallas kernels, run(): pl.pallas_call(functools.partial(kernel, replicas, models), out_shape=(V(...  170 us
    pallas_call x1, Pallas kernels, run(): pl.pallas_call(put, out_shape=tuple((jax.ShapeDtypeStruct(o.shape, o.dtyp...  8.02 us

profile of v2, /device:TPU:0, one launch (start us, length us, event | category | flops | bytes accessed | tf_op | source)
XLA Modules:
  0.0 179.1 jit_solution(2766118236619260099)
XLA Ops:
  0.6 170.4 %shard_map.143 = (bf16[2048,1536]{1,0:T(8,128)(2,1)S(1)}, bf16[2048,1536]{1,0:T(8,128)(2,1)S(1)}, bf16[1536,2048]{1,0:T(8,128)(2,1)S(1)}, f32[256,1536]{1,0:T(8,...) custom-call(f32[2,2,2,256,1536]{4,3,2,1,0:T(8,128)} %bitcast.7, ...), custom_call_target="tpu_custom_call" | custom-call | tf_op jit(solution)/shard_map/pallas_call | solution.py:525
  171.1 8.0 %shard_map.144 = (bf16[2048,1536]{1,0:T(8,128)(2,1)}, bf16[2048,1536]{1,0:T(8,128)(2,1)}, bf16[1536,2048]{1,0:T(8,128)(2,1)}, f32[256,1536]{1,0:T(8,128)}, f32[2...) custom-call(bf16[2048,1536]{1,0:T(8,128)(2,1)S(1)} %get-tuple-element.24.refs_0_, ...), custom_call_target="tpu_custom_call" | custom-call | tf_op jit(solution)/shard_map/pallas_call | solution.py:567

commit v3 on v2

--- a/solution.py
+++ b/solution.py
@@ -14,65 +14,37 @@
 PIECES = 2
 SLOTS = 2
 KERNEL_BYTES = 43000000
-OCTAVES = 252.0
-LOW = -125.0
-LN2 = 0.6931471805599453
+BEND = 15.0
+POWER = 63.0
+FLOOR = 125 * 0.6931471805599453
+TINY = 1e-30
 
 
 def tile_rows(columns, most=24576):
     return 16 * max(1, most // (16 * columns))
 
 
-def tiles(shape):
-    return [
-        (slice(r, r + 16), slice(c, c + 128))
-        for r in range(0, shape[0], 16)
-        for c in range(0, shape[1], 128)
-    ]
-
-
-def largest(t):
-    top = None
-    for r in range(0, t.shape[0], 8):
-        for c in range(0, t.shape[1], 128):
-            part = jnp.abs(t[r : r + 8, c : c + 128])
-            top = part if top is None else jnp.maximum(top, part)
-    return top
-
-
 def doubled(t):
     return jnp.concatenate([t, t], axis=0)
 
 
+def limit(top):
+    return (top * (1 + 2**-7)).astype(bf16)
+
+
 def encode(t, scale):
-    power = jnp.exp2(jnp.abs(t) * scale + LOW)
-    return jnp.where(t < 0, -power, power).astype(bf16)
-
-
-def decode(t, slope, base):
+    size = jnp.exp(POWER * jnp.log(1 + jnp.abs(t) * scale) - FLOOR)
+    return jnp.where(t < 0, -size, size).astype(bf16)
+
+
+def decode(t, scale):
     t = t.astype(f32)
-    size = jnp.log(jnp.abs(t)) * slope + base
+    size = (jnp.exp((jnp.log(jnp.abs(t)) + FLOOR) * (1 / POWER)) - 1) * scale
     return jnp.where(t < 0, -size, size)
 
 
-def encoder(top):
-    return doubled(OCTAVES / top)
-
-
-def decoder(top):
-    return doubled(top * (1.0 / (OCTAVES * LN2))), doubled(top * (-LOW / OCTAVES))
-
-
-def decode_block(ref, start, shape, code):
-    rows = []
-    for r in range(0, shape[0], 16):
-        at = pl.ds(pl.multiple_of(start + r, 16), 16)
-        rows.append(
-            jnp.concatenate(
-                [decode(ref[at, c : c + 128], *code) for c in range(0, shape[1], 128)], axis=1
-            )
-        )
-    return jnp.concatenate(rows, axis=0) if len(rows) > 1 else rows[0]
+def coded_at(row, column, wide):
+    return pl.ds(pl.multiple_of(row * wide + column * 16, 16), 16)
 
 
 def settle(copies):
@@ -84,12 +56,10 @@
     replicas, models,
     g_ref, u_ref, d_ref, pg_ref, pu_ref, pd_ref, sn_ref, pn_ref,
     hg_ref, hu_ref, hd_ref, ng_ref, nu_ref, nd_ref, hn_ref, nn_ref,
-    pr_g, pr_u, pr_d, r1_g, r1_u, r1_d, r2_g, r2_u, r2_d, pm_g, pm_u, pm_d,
-    c1_w, c1_d, c2_w, c2_d, ow_w, ow_d, top1, got1, top2, got2,
+    pr_g, pr_u, pr_d, pm_g, pm_u, pm_d, c1, r1, c2, r2, ow_w, ow_d,
     nrm_w, nrm_d, zs, zr_w, zr_d, ratios, nr, whole,
     ow_sem, pm_sem, pr_send, pr_recv, s1_send, s1_recv, s2_send, s2_recv,
-    t1_send, t1_recv, t2_send, t2_recv,
-    z_send, z_recv, n_send, n_recv, ag_send, ag_recv,
+    z_send, z_recv, n_send, n_recv, ag_send, ag_recv, ag_pair,
 ):
     me = lax.axis_index("replica")
     z = lax.axis_index("model")
@@ -104,7 +74,7 @@
     slopes = (g_ref, u_ref, d_ref)
     halves = (hg_ref, hu_ref, hd_ref)
     mn = (ng_ref, nu_ref, nd_ref)
-    pr, r1, r2 = (pr_g, pr_u, pr_d), (r1_g, r1_u, r1_d), (r2_g, r2_u, r2_d)
+    pr = (pr_g, pr_u, pr_d)
     params = (pm_g, pm_u, pm_d)
     units = 2 * PIECES
     side = nd_ref.shape[1]
@@ -128,12 +98,6 @@
             device_id=to, device_id_type=MESH,
         )
 
-    sent = []
-
-    def start(copy):
-        copy.start()
-        sent.append(copy)
-
     def height(m):
         return mn[m].shape[0] // units
 
@@ -153,14 +117,23 @@
     def own_copy(n, q):
         m, u = jobs[n]
         ow = ow_w if m < 2 else ow_d
-        return pltpu.make_async_copy(view(m, u, q, k), ow.at[n % SLOTS, q], ow_sem.at[m, u, q])
+        return pltpu.make_async_copy(view(m, u, q, k), ow.at[n % SLOTS, q], ow_sem.at[n % SLOTS, q])
 
     def pair_copy(n, q):
         m, u = jobs[n]
+        sem = 3 * n + min(q, 2) if n < units else 2 * units + n
         return remote(
-            view(m, u, q, 1 - k), pr[m].at[u, q],
-            pr_send.at[m, u, q], pr_recv.at[m, u, q], (partner, z),
-        )
+            view(m, u, q, 1 - k), pr[m].at[u, q], pr_send.at[m], pr_recv.at[sem], (partner, z)
+        )
+
+    def await_pair(n, q):
+        m, u = jobs[n]
+        if n < units:
+            at = pr[m].at[u, q] if q < 2 else pr[m].at[u, pl.ds(2, 2)]
+            settle([remote(at, at, pr_send.at[m], pr_recv.at[3 * n + q], (partner, z))])
+        elif q == 0:
+            at = pr[m].at[u]
+            settle([remote(at, at, pr_send.at[m], pr_recv.at[2 * units + n], (partner, z))])
 
     for n in range(SLOTS):
         for q in range(4):
@@ -174,44 +147,33 @@
 
     for q in range(2):
         for n in range(2):
-            start(pair_copy(n, q))
+            pair_copy(n, q).start()
     for n in range(2):
         for q in range(2, 4):
-            start(pair_copy(n, q))
+            pair_copy(n, q).start()
     for n in range(2, len(jobs)):
         for q in range(4):
-            start(pair_copy(n, q))
+            pair_copy(n, q).start()
     for copy in loads:
         copy.start()
 
-    def slot_of(n):
-        m = jobs[n][0]
-        return (c1_w, c2_w, n % units) if m < 2 else (c1_d, c2_d, n % units)
-
-    def first_copies(n, p):
-        m, u = jobs[n]
-        to = (xn if u < PIECES else yn, z)
-        c1, _, slot = slot_of(n)
-        return [
-            remote(
-                top1.at[m, u, p], got1.at[m, u, p], t1_send.at[m, u, p], t1_recv.at[m, u, p], to
-            ),
-            remote(
-                c1.at[slot, p], r1[m].at[u, p], s1_send.at[m, u, p], s1_recv.at[m, u, p], to
-            ),
-        ]
-
-    def second_copies(n):
-        m, u = jobs[n]
-        to = (yn if u < PIECES else xn, z)
-        _, c2, slot = slot_of(n)
-        return [
-            remote(top2.at[m, u], got2.at[m, u], t2_send.at[m, u], t2_recv.at[m, u], to),
-            remote(c2.at[slot], r2[m].at[u], s2_send.at[m, u], s2_recv.at[m, u], to),
-        ]
-
-    def reused(n):
-        return jobs[n][0] == 1
+    def first_copy(n, p):
+        m, u = jobs[n]
+        return remote(
+            c1.at[n % units, p], r1.at[m, u, p], s1_send.at[n % units, p],
+            s1_recv.at[n] if p == 0 else s2_recv.at[n], (xn if u < PIECES else yn, z),
+        )
+
+    def second_copy(n):
+        m, u = jobs[n]
+        return remote(
+            c2.at[n % units], r2.at[m, u], s2_send.at[n % units], s2_recv.at[n],
+            (yn if u < PIECES else xn, z),
+        )
+
+    def await_rest(n):
+        at = r1.at[jobs[n]]
+        settle([remote(at, at, s2_send.at[n % units], s2_recv.at[n], (xn, z))])
 
     def sweep(m, body, carry=None):
         step = tile_rows(mn[m].shape[1])
@@ -221,48 +183,106 @@
             return None
         return lax.fori_loop(0, trips, lambda i, c: body(i * step, step, c), carry)
 
-    def code_out(m, values, dst, top):
-        scale = encoder(top)
+    def code_rows(m, read, dst):
+        wide = mn[m].shape[1] // 128
+        lane = lax.broadcasted_iota(jnp.int32, (16, 128), 1)
+
+        def body(at, step, tops):
+            values = read(at, step)
+            for r in range(0, step, 16):
+                line = [values[r : r + 16, c * 128 : (c + 1) * 128] for c in range(wide)]
+                top = functools.reduce(jnp.maximum, [jnp.abs(t) for t in line])
+                top = jnp.maximum(jnp.max(top, axis=1, keepdims=True), TINY)
+                top = limit(jnp.broadcast_to(top, (16, 128))).astype(f32)
+                scale = BEND / top
+                for c, t in enumerate(line):
+                    dst[coded_at(at + r, c, wide), :] = encode(t, scale)
+                tops = jnp.where(lane == (at + r) // 16, top, tops)
+            return tops
+
+        tops = sweep(m, body, jnp.full((16, 128), TINY, f32))
+        dst[dst.shape[0] - 16 :, :] = tops.astype(bf16)
+
+    def code_columns(m, read, values, dst):
+        wide = mn[m].shape[1] // 128
+
+        def highest(at, step, tops):
+            t = jnp.abs(read(at, step))
+            for r in range(0, step, 8):
+                tops = jnp.maximum(tops, t[r : r + 8])
+            return tops
+
+        tops = sweep(m, highest, jnp.full((8, wide * 128), TINY, f32))
+        tops = limit(jnp.broadcast_to(jnp.max(tops, axis=0, keepdims=True), tops.shape))
+        tops = tops.astype(f32)
+        each = [tops[:, c * 128 : (c + 1) * 128] for c in range(wide)]
+        scales = [doubled(BEND / top) for top in each]
+        dst[dst.shape[0] - 16 :, :] = jnp.concatenate(each, axis=0).astype(bf16)
 
         def body(at, step):
             for r in range(0, step, 16):
                 rows = pl.ds(pl.multiple_of(at + r, 16), 16)
-                for c in range(0, mn[m].shape[1], 128):
-                    dst[rows, c : c + 128] = encode(values[rows, c : c + 128], scale)
+                for c in range(wide):
+                    t = values[rows, c * 128 : (c + 1) * 128]
+                    dst[coded_at(at + r, c, wide), :] = encode(t, scales[c])
 
         sweep(m, body)
 
-    blank = jnp.full((8, 128), 1e-30, f32)
+    def code_out(m, read, values, dst):
+        if m < 2:
+            code_rows(m, read, dst)
+        else:
+            code_columns(m, read, values, dst)
+
+    def scales_of(m, src, at):
+        tops = src[src.shape[0] - 16 :, :].astype(f32) * (1 / BEND)
+        wide = mn[m].shape[1] // 128
+        if m == 2:
+            each = [doubled(tops[c * 8 : (c + 1) * 8]) for c in range(wide)]
+            return lambda r: each
+        lane = lax.broadcasted_iota(jnp.int32, (16, 128), 1)
+
+        def of(r):
+            top = jnp.where(lane == (at + r) // 16, tops, 0)
+            return [jnp.broadcast_to(jnp.max(top, axis=1, keepdims=True), (16, 128))] * wide
+
+        return of
+
+    def decoded(m, src, at, step):
+        wide = mn[m].shape[1] // 128
+        of = scales_of(m, src, at)
+        rows = []
+        for r in range(0, step, 16):
+            scales = of(r)
+            line = [decode(src[coded_at(at + r, c, wide), :], scales[c]) for c in range(wide)]
+            rows.append(jnp.concatenate(line, axis=1))
+        return jnp.concatenate(rows, axis=0) if len(rows) > 1 else rows[0]
 
     def add(n, q, at, step):
         m, u = jobs[n]
         ow = ow_w if m < 2 else ow_d
         rows = pl.ds(pl.multiple_of(at, 16), step)
         both = pr[m][u, q, rows, :] + ow[n % SLOTS, q, rows, :]
-        pr[m][u, q, rows, :] = both
+        if m == 2 or q >= 2:
+            pr[m][u, q, rows, :] = both
         return both
 
     def stage_1(n, p):
         m, u = jobs[n]
         own_copy(n, p).wait()
-        settle([pair_copy(n, p)])
-        top = sweep(
-            m, lambda at, step, c: jnp.maximum(c, largest(add(n, p, at, step))), blank
-        )
-        top1[m, u, p] = top
-        c1, _, slot = slot_of(n)
-        if reused(n):
-            for copy in first_copies(n - units, p):
-                copy.wait_send()
-        code_out(m, pr[m].at[u, p], c1.at[slot, p], top)
-        for copy in first_copies(n, p):
-            copy.start()
+        await_pair(n, p)
+        if n >= units:
+            first_copy(n - units, p).wait_send()
+        code_out(
+            m, lambda at, step: add(n, p, at, step), pr[m].at[u, p], c1.at[n % units, p]
+        )
+        first_copy(n, p).start()
 
     def stage_1_rest(n):
         m, u = jobs[n]
+        await_pair(n, 2)
         for q in range(2, 4):
             own_copy(n, q).wait()
-            settle([pair_copy(n, q)])
 
             def keep(at, step):
                 add(n, q, at, step)
@@ -274,25 +294,19 @@
 
     def stage_2(n):
         m, u = jobs[n]
-        settle(first_copies(n, 0))
-        code = decoder(got1[m, u, 0])
-        columns = mn[m].shape[1]
-
-        def body(at, step, c):
+        settle([first_copy(n, 0)])
+
+        def both(at, step):
             rows = pl.ds(pl.multiple_of(at, 16), step)
-            both = pr[m][u, 2, rows, :] + decode_block(r1[m].at[u, 0], at, (step, columns), code)
-            pr[m][u, 2, rows, :] = both
-            return jnp.maximum(c, largest(both))
-
-        top = sweep(m, body, blank)
-        top2[m, u] = top
-        _, c2, slot = slot_of(n)
-        if reused(n):
-            for copy in second_copies(n - units):
-                copy.wait_send()
-        code_out(m, pr[m].at[u, 2], c2.at[slot], top)
-        for copy in second_copies(n):
-            copy.start()
+            total = pr[m][u, 2, rows, :] + decoded(m, r1.at[m, u, 0], at, step)
+            if m == 2:
+                pr[m][u, 2, rows, :] = total
+            return total
+
+        if n >= units:
+            second_copy(n - units).wait_send()
+        code_out(m, both, pr[m].at[u, 2], c2.at[n % units])
+        second_copy(n).start()
 
     def lanes(t):
         total = t[:, :128]
@@ -308,10 +322,7 @@
 
     def stage_3(n):
         m, u = jobs[n]
-        settle(first_copies(n, 1))
-        settle(second_copies(n))
-        columns = mn[m].shape[1]
-        near, far = decoder(got1[m, u, 1]), decoder(got2[m, u])
+        await_rest(n)
         if u == sequence[0]:
             loads[m].wait()
             if m == 2:
@@ -320,8 +331,8 @@
         def body(at, step):
             rows = pl.ds(pl.multiple_of(at, 16), step)
             here = pl.ds(pl.multiple_of(u * height(m) + at, 16), step)
-            mean = pr[m][u, 3, rows, :] + decode_block(r1[m].at[u, 1], at, (step, columns), near)
-            mean = (mean + decode_block(r2[m].at[u], at, (step, columns), far)) * rate
+            mean = pr[m][u, 3, rows, :] + decoded(m, r1.at[m, u, 1], at, step)
+            mean = (mean + decoded(m, r2.at[m, u], at, step)) * rate
             param = params[m][here, :]
             mn[m][here, :] = mean
             if m < 2:
@@ -338,10 +349,14 @@
         return [
             remote(
                 src, zr_w.at[m, n] if m < 2 else zr_d.at[n],
-                z_send.at[m, n], z_recv.at[m, n], (me, layer),
+                z_send.at[m], z_recv.at[m], (me, layer),
             )
             for n, layer in enumerate(layers)
         ]
+
+    def all_sizes(m):
+        at = zr_w.at[m] if m < 2 else zr_d
+        return remote(at, at, z_send.at[m], z_recv.at[m], (me, layers[0]))
 
     def send_sizes(m):
         if m < 2:
@@ -351,7 +366,7 @@
                     row = q * bands + b
                     zs[m, row : row + 1, :] = jnp.sum(block.T, axis=0, keepdims=True)
         for copy in size_copies(m):
-            start(copy)
+            copy.start()
 
     def piece(m, chip, core, h):
         ref = halves[m]
@@ -365,7 +380,16 @@
     chip, chip_x, chip_y, chip_d = me // 2, xn // 2, yn // 2, 3 - me // 2
 
     def gather(m, h, way, at, to):
-        return remote(at, at, ag_send.at[m, h, way], ag_recv.at[m, h, way], (to, z))
+        sem = ag_recv.at[m, h, way] if way < 3 else ag_pair.at[m]
+        return remote(at, at, ag_send.at[m], sem, (to, z))
+
+    def gathered(m, count):
+        rows, columns = mn[m].shape
+        if m < 2:
+            at = halves[m].at[pl.ds(0, rows * count // 2), :]
+        else:
+            at = halves[m].at[:, pl.ds(0, columns * count // 2)]
+        return remote(at, at, ag_send.at[m], ag_pair.at[m], (partner, z))
 
     def await_piece(m, h, way, chip_from, core):
         at = piece(m, chip_from, core, h)
@@ -373,7 +397,7 @@
         return at
 
     def update(m):
-        settle(size_copies(m))
+        settle([all_sizes(m)])
         if m == 2:
             both = nrm_d[...]
             for n in range(models - 1):
@@ -408,41 +432,40 @@
                 mn[m][rows, :] = new
                 at[here, :] = new.astype(bf16)
 
-            for way, to in ((1, xn), (2, yn), (0, partner)):
-                start(gather(m, h, way, at, to))
+            for way, to in ((0, xn), (1, yn), (3, partner)):
+                gather(m, h, way, at, to).start()
+
+    def relay(m, h, way, chip_from, *targets):
+        at = await_piece(m, h, way, chip_from, k)
+        for to_way, to in targets:
+            gather(m, h, to_way, at, to).start()
 
     def forward(m):
-        at = await_piece(m, 0, 1, chip_x, k)
-        start(gather(m, 0, 3, at, yn))
-        start(gather(m, 0, 4, at, partner))
-        at = await_piece(m, 1, 2, chip_y, k)
-        start(gather(m, 1, 3, at, xn))
-        start(gather(m, 1, 5, at, partner))
+        relay(m, 0, 0, chip_x, (2, yn), (3, partner))
+        relay(m, 1, 1, chip_y, (2, xn), (3, partner))
 
     def hand_over(m):
-        at = await_piece(m, 1, 1, chip_x, k)
-        start(gather(m, 1, 4, at, partner))
-        at = await_piece(m, 0, 2, chip_y, k)
-        start(gather(m, 0, 5, at, partner))
+        relay(m, 1, 0, chip_x, (3, partner))
+        relay(m, 0, 1, chip_y, (3, partner))
         for h in range(2):
-            at = await_piece(m, h, 3, chip_d, k)
-            start(gather(m, h, 6, at, partner))
+            relay(m, h, 2, chip_d, (3, partner))
 
     tall, share = hn_ref.shape[0], nn_ref.shape[0]
+
+    def all_vectors():
+        at = nr.at[pl.ds(0, replicas - 1)]
+        return remote(at, at, n_send.at[0], n_recv.at[0], (partner, z))
 
     def send_vectors():
         nr[me, :tall] = sn_ref[...]
         nr[me, tall:] = jnp.concatenate(
             [pn_ref[...], jnp.zeros((nr.shape[1] - tall - share, 128), f32)]
         )
-        for n, other in enumerate(others):
-            start(remote(nr.at[me], nr.at[me], n_send.at[n], n_recv.at[me], (other, z)))
+        for other in others:
+            remote(nr.at[me], nr.at[me], n_send.at[0], n_recv.at[0], (other, z)).start()
 
     def finish_vectors():
-        for d in range(1, replicas):
-            source = lax.rem(me + d, replicas)
-            at = nr.at[source]
-            settle([remote(at, at, n_send.at[d - 1], n_recv.at[source], (source, z))])
+        settle([all_vectors()])
         total = nr[0, :tall]
         for n in range(1, replicas):
             total = total + nr[n, :tall]
@@ -479,17 +502,16 @@
     for m in range(3):
         hand_over(m)
     for m in range(3):
-        for h in range(2):
-            await_piece(m, h, 0, chip, 1 - k)
-            await_piece(m, h, 4, chip_x, 1 - k)
-            await_piece(m, h, 5, chip_y, 1 - k)
-            await_piece(m, h, 6, chip_d, 1 - k)
-    for n in range(len(jobs)):
-        if n + units >= len(jobs) or not reused(n + units):
-            for copy in first_copies(n, 0) + first_copies(n, 1) + second_copies(n):
-                copy.wait_send()
-    for copy in sent:
-        copy.wait_send()
+        settle([gathered(m, replicas)])
+    for n in range(len(jobs) - units, len(jobs)):
+        for p in range(2):
+            first_copy(n, p).wait_send()
+        second_copy(n).wait_send()
+    for m in range(3):
+        remote(pr[m], pr[m], pr_send.at[m], pr_recv.at[0], (partner, z)).wait_send()
+        all_sizes(m).wait_send()
+        gathered(m, 2 * replicas - 2).wait_send()
+    all_vectors().wait_send()
 
 
 def put(*refs):
@@ -515,6 +537,7 @@
         tall_n, share = slope_norm.shape[1] // 128, param_norm.shape[0] // 128
         lines = tall_n + share + -(tall_n + share) % 8
         wide, deep = (rows // units, columns), (tall // units, side)
+        coded = (rows // units * columns // 128 + 16, 128)
         V, DMA = pltpu.VMEM, pltpu.SemaphoreType.DMA
         by_chip = (2, replicas // 4, 2, rows, columns)
         whole, inside = pl.BlockSpec(memory_space=pl.ANY), pl.BlockSpec(memory_space=pltpu.VMEM)
@@ -537,23 +560,19 @@
             in_specs=[whole] * 6 + [inside] * 2,
             out_specs=tuple([inside] * 8),
             scratch_shapes=[
-                *three((units, 4), f32), *three((units, 2), bf16), *three((units,), bf16),
+                *three((units, 4), f32),
                 V((rows, columns), f32), V((rows, columns), f32), V((tall, side), f32),
-                V((units, 2) + wide, bf16), V((units, 2) + deep, bf16),
-                V((units,) + wide, bf16), V((units,) + deep, bf16),
+                V((units, 2) + coded, bf16), V((3, units, 2) + coded, bf16),
+                V((units,) + coded, bf16), V((3, units) + coded, bf16),
                 V((SLOTS, 4) + wide, f32), V((SLOTS, 4) + deep, f32),
-                V((3, units, 2, 8, 128), f32), V((3, units, 2, 8, 128), f32),
-                V((3, units, 8, 128), f32), V((3, units, 8, 128), f32),
                 V((2, rows, 128), f32), V((2, 8, side), f32),
                 V((2, 2 * rows // 128, 128), f32), V((2, models - 1, 2 * rows // 128, 128), f32),
                 V((models - 1, 2, 8, side), f32), V((rows, 128), f32),
                 V((replicas, lines, 128), f32), V((tall_n, 128), f32),
-                DMA((3, units, 4)), DMA((3,)), DMA((3, units, 4)), DMA((3, units, 4)),
-                DMA((3, units, 2)), DMA((3, units, 2)), DMA((3, units)), DMA((3, units)),
-                DMA((3, units, 2)), DMA((3, units, 2)), DMA((3, units)), DMA((3, units)),
-                DMA((3, models - 1)), DMA((3, models - 1)),
-                DMA((replicas - 1,)), DMA((replicas,)),
-                DMA((3, 2, 7)), DMA((3, 2, 7)),
+                DMA((SLOTS, 4)), DMA((3,)), DMA((3,)), DMA((5 * units,)),
+                DMA((units, 2)), DMA((3 * units,)), DMA((units,)), DMA((3 * units,)),
+                DMA((3,)), DMA((3,)), DMA((1,)), DMA((1,)),
+                DMA((3,)), DMA((3, 2, 3)), DMA((3,)),
             ],
             compiler_params=pltpu.CompilerParams(
                 collective_id=0, has_side_effects=True, vmem_limit_bytes=KERNEL_BYTES

time: 179 us -> 177 us (0.989)
  Pallas kernels: 178 us -> 176 us
    pallas_call x1, Pallas kernels: 170 us -> 168 us  [run(): pl.pallas_call(functools.partial(kernel, replicas, models), out_shape=(V(...]
where the time goes in v3:
time: 177 us
  Pallas kernels  176 us (99%)
    pallas_call x1, Pallas kernels, run(): pl.pallas_call(functools.partial(kernel, replicas, models), out_shape=(V(...  168 us
    pallas_call x1, Pallas kernels, run(): pl.pallas_call(put, out_shape=tuple((jax.ShapeDtypeStruct(o.shape, o.dtyp...  8.02 us

profile of v3, /device:TPU:0, one launch (start us, length us, event | category | flops | bytes accessed | tf_op | source)
XLA Modules:
  0.0 176.6 jit_solution(7101059616186668442)
XLA Ops:
  0.6 167.9 %shard_map.143 = (bf16[2048,1536]{1,0:T(8,128)(2,1)S(1)}, bf16[2048,1536]{1,0:T(8,128)(2,1)S(1)}, bf16[1536,2048]{1,0:T(8,128)(2,1)S(1)}, f32[256,1536]{1,0:T(8,...) custom-call(f32[2,2,2,256,1536]{4,3,2,1,0:T(8,128)} %bitcast.7, ...), custom_call_target="tpu_custom_call" | custom-call | tf_op jit(solution)/shard_map/pallas_call | solution.py:548
  168.6 8.0 %shard_map.144 = (bf16[2048,1536]{1,0:T(8,128)(2,1)}, bf16[2048,1536]{1,0:T(8,128)(2,1)}, bf16[1536,2048]{1,0:T(8,128)(2,1)}, f32[256,1536]{1,0:T(8,128)}, f32[2...) custom-call(bf16[2048,1536]{1,0:T(8,128)(2,1)S(1)} %get-tuple-element.24.refs_0_, ...), custom_call_target="tpu_custom_call" | custom-call | tf_op jit(solution)/shard_map/pallas_call | solution.py:586

commit v4 on v3

--- a/solution.py
+++ b/solution.py
@@ -18,6 +18,7 @@
 POWER = 63.0
 FLOOR = 125 * 0.6931471805599453
 TINY = 1e-30
+CUTS = 2
 
 
 def tile_rows(columns, most=24576):
@@ -57,9 +58,9 @@
     g_ref, u_ref, d_ref, pg_ref, pu_ref, pd_ref, sn_ref, pn_ref,
     hg_ref, hu_ref, hd_ref, ng_ref, nu_ref, nd_ref, hn_ref, nn_ref,
     pr_g, pr_u, pr_d, pm_g, pm_u, pm_d, c1, r1, c2, r2, ow_w, ow_d,
-    nrm_w, nrm_d, zs, zr_w, zr_d, ratios, nr, whole,
+    nrm_w, nrm_d, zs_w, zr_w, zs_d, zr_d, ratios, vs, vr, whole,
     ow_sem, pm_sem, pr_send, pr_recv, s1_send, s1_recv, s2_send, s2_recv,
-    z_send, z_recv, n_send, n_recv, ag_send, ag_recv, ag_pair,
+    z_send, z_recv, v_send, v_recv, ag_send, ag_recv, ag_pair,
 ):
     me = lax.axis_index("replica")
     z = lax.axis_index("model")
@@ -80,13 +81,11 @@
     side = nd_ref.shape[1]
     bands = ng_ref.shape[0] // 128
 
-    others = [lax.rem(me + d, replicas) for d in range(1, replicas)]
-    layers = [lax.rem(z + d, models) for d in range(1, models)]
+    near, far = z + 1 - 2 * lax.rem(z, 2), z + 2 - 4 * (z // 2)
     barrier = pltpu.get_barrier_semaphore()
-    for other in others:
-        pl.semaphore_signal(barrier, inc=1, device_id=(other, z), device_id_type=MESH)
-    for layer in layers:
-        pl.semaphore_signal(barrier, inc=1, device_id=(me, layer), device_id_type=MESH)
+    around = [(partner, z), (xn, z), (yn, z), (me, near), (me, far)]
+    for to in around:
+        pl.semaphore_signal(barrier, inc=1, device_id=to, device_id_type=MESH)
 
     sequence = [h * PIECES + j for j in range(PIECES) for h in range(2)]
     jobs = [(m, u) for m in range(3) for u in sequence]
@@ -143,7 +142,29 @@
         for m, src in enumerate((pg_ref, pu_ref, pd_ref))
     ]
 
-    pl.semaphore_wait(barrier, replicas - 1 + models - 1)
+    tall, share = hn_ref.shape[0], nn_ref.shape[0]
+
+    def vector_copy(step):
+        to = (partner, xn, yn)[step]
+        return remote(vs.at[step], vr.at[step], v_send.at[step], v_recv.at[step], (to, z))
+
+    def send_vectors(step):
+        if step == 0:
+            line = lax.broadcasted_iota(jnp.int32, (tall, 128), 0)
+            params_of_all = jnp.concatenate([pn_ref[...]] * replicas)
+            vs[0, :tall] = sn_ref[...]
+            vs[0, tall:] = jnp.where(line // share == me, params_of_all, 0)
+        else:
+            vs[step] = sum_vectors(step - 1)
+        vector_copy(step).start()
+
+    def sum_vectors(step):
+        settle([vector_copy(step)])
+        return vs[step] + vr[step]
+
+    pl.semaphore_wait(barrier, len(around))
+
+    send_vectors(0)
 
     for q in range(2):
         for n in range(2):
@@ -344,19 +365,14 @@
 
         sweep(m, body)
 
-    def size_copies(m):
-        src = zs.at[m] if m < 2 else nrm_d
-        return [
-            remote(
-                src, zr_w.at[m, n] if m < 2 else zr_d.at[n],
-                z_send.at[m], z_recv.at[m], (me, layer),
-            )
-            for n, layer in enumerate(layers)
-        ]
-
-    def all_sizes(m):
-        at = zr_w.at[m] if m < 2 else zr_d
-        return remote(at, at, z_send.at[m], z_recv.at[m], (me, layers[0]))
+    def sizes(m, step):
+        out, back = (zs_w.at[m], zr_w.at[m]) if m < 2 else (zs_d, zr_d)
+        return out.at[step], back.at[step]
+
+    def size_copy(m, step):
+        out, back = sizes(m, step)
+        to = (me, near if step == 0 else far)
+        return remote(out, back, z_send.at[m, step], z_recv.at[m, step], to)
 
     def send_sizes(m):
         if m < 2:
@@ -364,9 +380,20 @@
                 for b in range(bands):
                     block = nrm_w[q, b * 128 : (b + 1) * 128, :]
                     row = q * bands + b
-                    zs[m, row : row + 1, :] = jnp.sum(block.T, axis=0, keepdims=True)
-        for copy in size_copies(m):
-            copy.start()
+                    zs_w[m, 0, row : row + 1, :] = jnp.sum(block.T, axis=0, keepdims=True)
+        else:
+            zs_d[0] = nrm_d[...]
+        size_copy(m, 0).start()
+
+    def all_sizes(m, step):
+        settle([size_copy(m, step)])
+        out, back = sizes(m, step)
+        return out[...] + back[...]
+
+    def relay_sizes(m):
+        both = all_sizes(m, 0)
+        sizes(m, 1)[0][...] = both
+        size_copy(m, 1).start()
 
     def piece(m, chip, core, h):
         ref = halves[m]
@@ -397,19 +424,13 @@
         return at
 
     def update(m):
-        settle([all_sizes(m)])
+        total = all_sizes(m, 1)
         if m == 2:
-            both = nrm_d[...]
-            for n in range(models - 1):
-                both = both + zr_d[n]
-            own = jnp.sum(both[0], axis=0, keepdims=True)
-            size = jnp.sum(both[1], axis=0, keepdims=True)
+            own = jnp.sum(total[0], axis=0, keepdims=True)
+            size = jnp.sum(total[1], axis=0, keepdims=True)
             ratio_d = jnp.sqrt(own) * lax.rsqrt(size + eps)
         else:
-            both = zs[m]
-            for n in range(models - 1):
-                both = both + zr_w[m, n]
-            ratio = jnp.sqrt(both[:bands]) * lax.rsqrt(both[bands : 2 * bands] + eps)
+            ratio = jnp.sqrt(total[:bands]) * lax.rsqrt(total[bands : 2 * bands] + eps)
             for b in range(bands):
                 ratios[b * 128 : (b + 1) * 128, :] = jnp.broadcast_to(
                     ratio[b : b + 1], (128, 128)
@@ -450,28 +471,9 @@
         for h in range(2):
             relay(m, h, 2, chip_d, (3, partner))
 
-    tall, share = hn_ref.shape[0], nn_ref.shape[0]
-
-    def all_vectors():
-        at = nr.at[pl.ds(0, replicas - 1)]
-        return remote(at, at, n_send.at[0], n_recv.at[0], (partner, z))
-
-    def send_vectors():
-        nr[me, :tall] = sn_ref[...]
-        nr[me, tall:] = jnp.concatenate(
-            [pn_ref[...], jnp.zeros((nr.shape[1] - tall - share, 128), f32)]
-        )
-        for other in others:
-            remote(nr.at[me], nr.at[me], n_send.at[0], n_recv.at[0], (other, z)).start()
-
     def finish_vectors():
-        settle([all_vectors()])
-        total = nr[0, :tall]
-        for n in range(1, replicas):
-            total = total + nr[n, :tall]
-        for n in range(replicas):
-            rows = slice(n * share, (n + 1) * share)
-            whole[rows, :] = nr[n, tall : tall + share] - learn_rate * (total[rows] * rate)
+        total = sum_vectors(2)
+        whole[...] = total[tall:] - learn_rate * (total[:tall] * rate)
         hn_ref[...] = whole[...].astype(bf16)
         nn_ref[...] = whole[pl.ds(me * share, share), :]
 
@@ -482,19 +484,25 @@
                     stage_1(n, p)
             for n in (2 * t, 2 * t + 1):
                 stage_1_rest(n)
-        if t == 0:
-            send_vectors()
-        for stage, lag in ((stage_2, 1), (stage_3, 2)):
-            if 0 <= t - lag < steps:
-                for n in (2 * (t - lag), 2 * (t - lag) + 1):
-                    stage(n)
+        due, rest = divmod(t - 2, PIECES)
+        updates = t > 2 and rest == 0 and 1 <= due <= 2
+        if 0 <= t - 1 < steps:
+            stage_2(2 * t - 2)
+            stage_2(2 * t - 1)
+        if updates:
+            relay_sizes(due - 1)
+        if 0 <= t - 2 < steps:
+            stage_3(2 * t - 4)
+            stage_3(2 * t - 3)
         done, rest = divmod(t - 2 + 1, PIECES)
         if t >= 2 and rest == 0 and done >= 1:
             send_sizes(done - 1)
-        done, rest = divmod(t - 2, PIECES)
-        if t > 2 and rest == 0 and 1 <= done <= 2:
-            update(done - 1)
+        if updates:
+            update(due - 1)
+        if t in (2, 5):
+            send_vectors(t // 2)
     forward(0)
+    relay_sizes(2)
     update(2)
     finish_vectors()
     forward(1)
@@ -509,18 +517,22 @@
         second_copy(n).wait_send()
     for m in range(3):
         remote(pr[m], pr[m], pr_send.at[m], pr_recv.at[0], (partner, z)).wait_send()
-        all_sizes(m).wait_send()
+        for step in range(2):
+            size_copy(m, step).wait_send()
         gathered(m, 2 * replicas - 2).wait_send()
-    all_vectors().wait_send()
+    for step in range(3):
+        vector_copy(step).wait_send()
 
 
 def put(*refs):
     count = len(refs) // 2
-    ins, outs, sem = refs[:count], refs[count : 2 * count], refs[2 * count]
-    copies = [
-        pltpu.make_async_copy(src, dst, sem.at[n])
-        for n, (src, dst) in enumerate(zip(ins, outs))
-    ]
+    copies = []
+    for n, (src, dst) in enumerate(zip(refs[:count], refs[count : 2 * count])):
+        rows = src.shape[0]
+        tall = rows // CUTS if rows % (32 * CUTS) == 0 else rows
+        for c in range(rows // tall):
+            at = pl.ds(c * tall, tall)
+            copies.append(pltpu.make_async_copy(src.at[at], dst.at[at], refs[-1].at[n, c]))
     for copy in copies:
         copy.start()
     for copy in copies:
@@ -535,7 +547,6 @@
         tall, side = param_down.shape
         units = 2 * PIECES
         tall_n, share = slope_norm.shape[1] // 128, param_norm.shape[0] // 128
-        lines = tall_n + share + -(tall_n + share) % 8
         wide, deep = (rows // units, columns), (tall // units, side)
         coded = (rows // units * columns // 128 + 16, 128)
         V, DMA = pltpu.VMEM, pltpu.SemaphoreType.DMA
@@ -566,12 +577,12 @@
                 V((units,) + coded, bf16), V((3, units) + coded, bf16),
                 V((SLOTS, 4) + wide, f32), V((SLOTS, 4) + deep, f32),
                 V((2, rows, 128), f32), V((2, 8, side), f32),
-                V((2, 2 * rows // 128, 128), f32), V((2, models - 1, 2 * rows // 128, 128), f32),
-                V((models - 1, 2, 8, side), f32), V((rows, 128), f32),
-                V((replicas, lines, 128), f32), V((tall_n, 128), f32),
+                V((2, 2, 2 * rows // 128, 128), f32), V((2, 2, 2 * rows // 128, 128), f32),
+                V((2, 2, 8, side), f32), V((2, 2, 8, side), f32), V((rows, 128), f32),
+                V((3, 2 * tall_n, 128), f32), V((3, 2 * tall_n, 128), f32), V((tall_n, 128), f32),
                 DMA((SLOTS, 4)), DMA((3,)), DMA((3,)), DMA((5 * units,)),
                 DMA((units, 2)), DMA((3 * units,)), DMA((units,)), DMA((3 * units,)),
-                DMA((3,)), DMA((3,)), DMA((1,)), DMA((1,)),
+                DMA((3, 2)), DMA((3, 2)), DMA((3,)), DMA((3,)),
                 DMA((3,)), DMA((3, 2, 3)), DMA((3,)),
             ],
             compiler_params=pltpu.CompilerParams(
@@ -588,7 +599,7 @@
                 out_shape=tuple(jax.ShapeDtypeStruct(o.shape, o.dtype) for o in out),
                 in_specs=[inside] * len(out),
                 out_specs=tuple([whole] * len(out)),
-                scratch_shapes=[DMA((len(out),))],
+                scratch_shapes=[DMA((len(out), CUTS))],
                 compiler_params=pltpu.CompilerParams(vmem_limit_bytes=1 << 20),
             )(*[pltpu.with_memory_space_constraint(o, pltpu.VMEM) for o in out])
         )
@@ -628,7 +639,7 @@
 
 def solution(mesh):
     replicas, models = mesh.shape["replica"], mesh.shape["model"]
-    body = fused(replicas, models) if replicas == 2 * 2 * 2 else plain
+    body = fused(replicas, models) if replicas == 2 * 2 * 2 and models == 4 else plain
     matrix, turned = P("replica", "model"), P("model", "replica")
     return jax.shard_map(
         body,

time: 177 us -> 175 us (0.989)
  Pallas kernels: 176 us -> 174 us
where the time goes in v4:
time: 175 us
  Pallas kernels  174 us (99%)
    pallas_call x1, Pallas kernels, run(): pl.pallas_call(functools.partial(kernel, replicas, models), out_shape=(V(...  166 us
    pallas_call x1, Pallas kernels, run(): pl.pallas_call(put, out_shape=tuple((jax.ShapeDtypeStruct(o.shape, o.dtyp...  8.07 us

profile of v4, /device:TPU:0, one launch (start us, length us, event | category | flops | bytes accessed | tf_op | source)
XLA Modules:
  0.0 175.0 jit_solution(6021543255650856868)
XLA Ops:
  0.6 166.3 %shard_map.143 = (bf16[2048,1536]{1,0:T(8,128)(2,1)S(1)}, bf16[2048,1536]{1,0:T(8,128)(2,1)S(1)}, bf16[1536,2048]{1,0:T(8,128)(2,1)S(1)}, f32[256,1536]{1,0:T(8,...) custom-call(f32[2,2,2,256,1536]{4,3,2,1,0:T(8,128)} %bitcast.7, ...), custom_call_target="tpu_custom_call" | custom-call | tf_op jit(solution)/shard_map/pallas_call | solution.py:559
  167.0 8.1 %shard_map.144 = (bf16[2048,1536]{1,0:T(8,128)(2,1)}, bf16[2048,1536]{1,0:T(8,128)(2,1)}, bf16[1536,2048]{1,0:T(8,128)(2,1)}, f32[256,1536]{1,0:T(8,128)}, f32[2...) custom-call(bf16[2048,1536]{1,0:T(8,128)(2,1)S(1)} %get-tuple-element.24.refs_0_, ...), custom_call_target="tpu_custom_call" | custom-call | tf_op jit(solution)/shard_map/pallas_call | solution.py:597

commit v5 on v4

--- a/solution.py
+++ b/solution.py
@@ -59,7 +59,7 @@
     hg_ref, hu_ref, hd_ref, ng_ref, nu_ref, nd_ref, hn_ref, nn_ref,
     pr_g, pr_u, pr_d, pm_g, pm_u, pm_d, c1, r1, c2, r2, ow_w, ow_d,
     nrm_w, nrm_d, zs_w, zr_w, zs_d, zr_d, ratios, vs, vr, whole,
-    ow_sem, pm_sem, pr_send, pr_recv, s1_send, s1_recv, s2_send, s2_recv,
+    st_sem, ow_sem, pm_sem, pr_send, pr_recv, s1_send, s1_recv, s2_send, s2_recv,
     z_send, z_recv, v_send, v_recv, ag_send, ag_recv, ag_pair,
 ):
     me = lax.axis_index("replica")
@@ -134,6 +134,18 @@
             at = pr[m].at[u]
             settle([remote(at, at, pr_send.at[m], pr_recv.at[2 * units + n], (partner, z))])
 
+    def staged(i):
+        n, q = i % 2, i // 2
+        m, u = jobs[n]
+        at = mn[m].at[pl.ds(i * height(m), height(m)), :]
+        here = pltpu.make_async_copy(view(m, u, q, 1 - k), at, st_sem.at[i])
+        there = remote(
+            at, pr[m].at[u, q], pr_send.at[3], pr_recv.at[3 * n + q], (partner, z)
+        )
+        return here, there
+
+    for i in range(4):
+        staged(i)[0].start()
     for n in range(SLOTS):
         for q in range(4):
             own_copy(n, q).start()
@@ -166,9 +178,10 @@
 
     send_vectors(0)
 
-    for q in range(2):
-        for n in range(2):
-            pair_copy(n, q).start()
+    for i in range(4):
+        here, there = staged(i)
+        here.wait()
+        there.start()
     for n in range(2):
         for q in range(2, 4):
             pair_copy(n, q).start()
@@ -346,6 +359,8 @@
         await_rest(n)
         if u == sequence[0]:
             loads[m].wait()
+            if m == 0:
+                remote(mn[0], mn[0], pr_send.at[3], pr_recv.at[0], (partner, z)).wait_send()
             if m == 2:
                 nrm_d[...] = jnp.zeros_like(nrm_d)
 
@@ -516,7 +531,8 @@
             first_copy(n, p).wait_send()
         second_copy(n).wait_send()
     for m in range(3):
-        remote(pr[m], pr[m], pr_send.at[m], pr_recv.at[0], (partner, z)).wait_send()
+        at = pr[m].at[pl.ds(0, units - 1)] if m == 0 else pr[m]
+        remote(at, at, pr_send.at[m], pr_recv.at[0], (partner, z)).wait_send()
         for step in range(2):
             size_copy(m, step).wait_send()
         gathered(m, 2 * replicas - 2).wait_send()
@@ -580,7 +596,7 @@
                 V((2, 2, 2 * rows // 128, 128), f32), V((2, 2, 2 * rows // 128, 128), f32),
                 V((2, 2, 8, side), f32), V((2, 2, 8, side), f32), V((rows, 128), f32),
                 V((3, 2 * tall_n, 128), f32), V((3, 2 * tall_n, 128), f32), V((tall_n, 128), f32),
-                DMA((SLOTS, 4)), DMA((3,)), DMA((3,)), DMA((5 * units,)),
+                DMA((4,)), DMA((SLOTS, 4)), DMA((3,)), DMA((4,)), DMA((5 * units,)),
                 DMA((units, 2)), DMA((3 * units,)), DMA((units,)), DMA((3 * units,)),
                 DMA((3, 2)), DMA((3, 2)), DMA((3,)), DMA((3,)),
                 DMA((3,)), DMA((3, 2, 3)), DMA((3,)),

time: 175 us -> 175 us (level)
  no operation moved by 1% of the time
where the time goes in v5:
time: 175 us
  Pallas kernels  174 us (99%)
    pallas_call x1, Pallas kernels, run(): pl.pallas_call(functools.partial(kernel, replicas, models), out_shape=(V(...  166 us
    pallas_call x1, Pallas kernels, run(): pl.pallas_call(put, out_shape=tuple((jax.ShapeDtypeStruct(o.shape, o.dtyp...  8.07 us

profile of v5, /device:TPU:0, one launch (start us, length us, event | category | flops | bytes accessed | tf_op | source)
XLA Modules:
  0.0 174.9 jit_solution(2306145979294337043)
XLA Ops:
  0.6 166.2 %shard_map.143 = (bf16[2048,1536]{1,0:T(8,128)(2,1)S(1)}, bf16[2048,1536]{1,0:T(8,128)(2,1)S(1)}, bf16[1536,2048]{1,0:T(8,128)(2,1)S(1)}, f32[256,1536]{1,0:T(8,...) custom-call(f32[2,2,2,256,1536]{4,3,2,1,0:T(8,128)} %bitcast.7, ...), custom_call_target="tpu_custom_call" | custom-call | tf_op jit(solution)/shard_map/pallas_call | solution.py:575
  166.8 8.1 %shard_map.144 = (bf16[2048,1536]{1,0:T(8,128)(2,1)}, bf16[2048,1536]{1,0:T(8,128)(2,1)}, bf16[1536,2048]{1,0:T(8,128)(2,1)}, f32[256,1536]{1,0:T(8,128)}, f32[2...) custom-call(bf16[2048,1536]{1,0:T(8,128)(2,1)S(1)} %get-tuple-element.24.refs_0_, ...), custom_call_target="tpu_custom_call" | custom-call | tf_op jit(solution)/shard_map/pallas_call | solution.py:613
